TPU v7x, 32 devices: a whole 2x2x4 slice. The times are simulated.
32 devices in a mesh: dp: 16 (over z, y, x), tensor: 2 (over core).
Axes of the slice: x: 2, y: 2, z: 4, core: 2. Of those that a mesh axis runs over, the one named last changes fastest.
Arguments:
- tokens: bfloat16 [16384, 640], P('dp'), may hold values from -6 to 6
- cotangent: bfloat16 [16384, 640], P('dp'), may hold values from -6 to 6
- lengths: int32 [16], P('dp'), may hold values from 256 to 1024, as said below
- pad_mask: int32 [16, 1024], P('dp'), may hold values 0 or 1
- w_qkv: bfloat16 [640, 3, 640], P(None, None, 'tensor'), may hold values from -0.25 to 0.25
- b_qkv: float32 [3, 640], P(None, 'tensor'), may hold values from -3 to 3
- w_out: bfloat16 [640, 640], P('tensor'), may hold values from -4 to 4
- b_out: float32 [640], replicated, may hold values from -3 to 3
- w_up: bfloat16 [640, 2560], P(None, 'tensor'), may hold values from -0.25 to 0.25
- b_up: float32 [2560], P('tensor'), may hold values from -3 to 3
- w_down: bfloat16 [2560, 640], P('tensor'), may hold values from -0.125 to 0.125
- b_down: float32 [640], replicated, may hold values from -3 to 3
- gain_one: float32 [640], replicated, may hold values from 0.25 to 1.75
- shift_one: float32 [640], replicated, may hold values from -3 to 3
- gain_two: float32 [640], replicated, may hold values from 0.25 to 1.75
- shift_two: float32 [640], replicated, may hold values from -3 to 3
Outputs:
- out_tokens: bfloat16 [16384, 640], P('dp')
- grad_tokens: float32 [16384, 640], P('dp')
- grad_w_qkv: float32 [640, 3, 640], P(None, None, 'tensor')
- grad_b_qkv: float32 [3, 640], P(None, 'tensor')
- grad_w_out: float32 [640, 640], P('tensor')
- grad_b_out: float32 [640], replicated
- grad_w_up: float32 [640, 2560], P(None, 'tensor')
- grad_b_up: float32 [2560], P('tensor')
- grad_w_down: float32 [2560, 640], P('tensor')
- grad_b_down: float32 [640], replicated
- grad_gain_one: float32 [640], replicated
- grad_shift_one: float32 [640], replicated
- grad_gain_two: float32 [640], replicated
- grad_shift_two: float32 [640], replicated
Inputs may be any that keep to these rules, and one draw needn't show every extreme that they name: `lengths`: some window has exactly 1024 valid tokens and another exactly 256.
All inputs are finite; a program needn't handle non-finite values. No bound on the sum of `pad_mask` on one device may be relied on, other than what follows from the above.
Results may differ from a plain program's by a relative error of at most 0.012.
The roundings to bfloat16 on the way count: a program that leaves them out, or rounds other values in their place, can miss the bound.
Values sent between devices are 32-bit elements; how exact they have to be, the bound alone decides.
No kernel may reach another device: no remote copies, remote signals or barrier semaphores. Data moves between devices by JAX's collectives and lax.ppermute only.
A program may use at most 192 MiB of HBM per device.

v0:
```python
import jax
import jax.numpy as jnp
from jax import lax
from jax.sharding import PartitionSpec as P

HD = 32


EPSILON = 1e-05
ROOT_HALF = 0.7071067811865476
ROOT_TWO_PI = 2.5066282746310002


def normalize(values):
    centre = jnp.mean(values, axis=1, keepdims=True)
    shifted = values - centre
    inverse = lax.rsqrt(jnp.mean(shifted * shifted, axis=1, keepdims=True) + EPSILON)
    return (shifted * inverse, inverse)


def norm_back(grad_normed, normed, inverse, gain_vec):
    scaled = grad_normed * gain_vec
    first_mean = jnp.mean(scaled, axis=1, keepdims=True)
    second_mean = jnp.mean(scaled * normed, axis=1, keepdims=True)
    return inverse * (scaled - first_mean - normed * second_mean)


def rotate(values, cosine_table, sine_table):
    half_size = values.shape[-1] // 2
    lower_half = values[..., :half_size]
    upper_half = values[..., half_size:]
    turned = jnp.concatenate([-upper_half, lower_half], axis=-1)
    return values * cosine_table + turned * sine_table


def rotate_back(grads, cosine_table, sine_table):
    half_size = grads.shape[-1] // 2
    along = grads * sine_table
    lower_half = along[..., :half_size]
    upper_half = along[..., half_size:]
    return grads * cosine_table + jnp.concatenate([upper_half, -lower_half], axis=-1)


def attend_sequence(query_rows, key_rows, value_rows, visible):
    block_rows = min(512, query_rows.shape[0])
    block_count = query_rows.shape[0] // block_rows
    query_blocks = query_rows.reshape(
        block_count, block_rows, query_rows.shape[1], query_rows.shape[2]
    )

    def one_block(query_block):
        scores = jnp.einsum(
            "qhd,khd->hqk", query_block, key_rows, preferred_element_type=jnp.float32
        )
        scores = jnp.where(visible[None, None, :], scores, -1000000000.0)
        row_peak = jnp.max(scores, axis=2, keepdims=True)
        powers = jnp.exp(scores - row_peak)
        totals = jnp.sum(powers, axis=2, keepdims=True)
        chances = (powers / totals).astype(jnp.bfloat16)
        attended = jnp.einsum(
            "hqk,khd->qhd", chances, value_rows, preferred_element_type=jnp.float32
        )
        return (attended, (row_peak + jnp.log(totals))[:, :, 0])

    attended, log_norm = lax.map(one_block, query_blocks)
    return (attended.reshape(query_rows.shape), log_norm)


def attend_back(query_rows, key_rows, value_rows, visible, log_norm, grad_attended):
    block_rows = min(512, query_rows.shape[0])
    block_count = query_rows.shape[0] // block_rows
    query_blocks = query_rows.reshape(
        block_count, block_rows, query_rows.shape[1], query_rows.shape[2]
    )
    grad_blocks = grad_attended.reshape(
        block_count, block_rows, query_rows.shape[1], query_rows.shape[2]
    )

    def one_block(running, packed):
        grad_keys, grad_values = running
        query_block, grad_block, norm_block = packed
        scores = jnp.einsum(
            "qhd,khd->hqk", query_block, key_rows, preferred_element_type=jnp.float32
        )
        scores = jnp.where(visible[None, None, :], scores, -1000000000.0)
        chances = jnp.exp(scores - norm_block[:, :, None])
        grad_chances = jnp.einsum(
            "qhd,khd->hqk", grad_block, value_rows, preferred_element_type=jnp.float32
        )
        inner = jnp.sum(chances * grad_chances, axis=2, keepdims=True)
        grad_scores = (chances * (grad_chances - inner)).astype(jnp.bfloat16)
        grad_query = jnp.einsum(
            "hqk,khd->qhd", grad_scores, key_rows, preferred_element_type=jnp.float32
        )
        grad_keys = grad_keys + jnp.einsum(
            "hqk,qhd->khd", grad_scores, query_block, preferred_element_type=jnp.float32
        )
        grad_values = grad_values + jnp.einsum(
            "hqk,qhd->khd",
            chances.astype(jnp.bfloat16),
            grad_block,
            preferred_element_type=jnp.float32,
        )
        return ((grad_keys, grad_values), grad_query)

    empty_grads = jnp.zeros(key_rows.shape, jnp.float32)
    (grad_keys, grad_values), grad_query = lax.scan(
        one_block, (empty_grads, empty_grads), (query_blocks, grad_blocks, log_norm)
    )
    return (grad_query.reshape(query_rows.shape), grad_keys, grad_values)


def per_device(
    tokens,
    cotangent,
    lengths,
    pad_mask,
    w_qkv,
    b_qkv,
    w_out,
    b_out,
    w_up,
    b_up,
    w_down,
    b_down,
    gain_one,
    shift_one,
    gain_two,
    shift_two,
):
    row_count, model_width = tokens.shape
    seq_count = lengths.shape[0]
    seq_len = row_count // seq_count
    local_width = w_qkv.shape[2]
    head_count = local_width // HD
    query_scale = HD ** (-0.5)
    half_size = HD // 2
    frequency = 10000.0 ** (-(2.0 * jnp.arange(half_size, dtype=jnp.float32)) / HD)
    position = jnp.arange(seq_len, dtype=jnp.float32)[None, :]
    angles = position.reshape(row_count)[:, None] * frequency[None, :]
    cosine_table = jnp.concatenate([jnp.cos(angles), jnp.cos(angles)], axis=-1)[:, None, :]
    sine_table = jnp.concatenate([jnp.sin(angles), jnp.sin(angles)], axis=-1)[:, None, :]
    places = jnp.arange(seq_len, dtype=jnp.int32)[None, :]
    visible = (places < lengths[:, None]) & (pad_mask == 1) | (places == 0)
    inputs = tokens.astype(jnp.float32)
    normed_one, inverse_one = normalize(inputs)
    hidden_one = (normed_one * gain_one + shift_one).astype(jnp.bfloat16)
    flat_qkv = w_qkv.reshape(model_width, 3 * local_width)
    projected = jnp.dot(hidden_one, flat_qkv, preferred_element_type=jnp.float32) + b_qkv.reshape(
        -1
    )
    projected = projected.reshape(row_count, 3, head_count, HD)
    query_rows = (rotate(projected[:, 0], cosine_table, sine_table) * query_scale).astype(
        jnp.bfloat16
    )
    key_rows = rotate(projected[:, 1], cosine_table, sine_table).astype(jnp.bfloat16)
    value_rows = projected[:, 2].astype(jnp.bfloat16)
    seq_shape = (seq_count, seq_len, head_count, HD)
    query_seqs = query_rows.reshape(seq_shape)
    key_seqs = key_rows.reshape(seq_shape)
    value_seqs = value_rows.reshape(seq_shape)
    attended, log_norm = lax.map(
        lambda packed: attend_sequence(*packed), (query_seqs, key_seqs, value_seqs, visible)
    )
    attended_low = attended.reshape(row_count, local_width).astype(jnp.bfloat16)
    mix_part = jnp.dot(attended_low, w_out, preferred_element_type=jnp.float32)
    mix_total = lax.psum(mix_part, "tensor")
    resid_one = inputs + (mix_total + b_out)
    normed_two, inverse_two = normalize(resid_one)
    hidden_two = (normed_two * gain_two + shift_two).astype(jnp.bfloat16)
    upward = jnp.dot(hidden_two, w_up, preferred_element_type=jnp.float32) + b_up
    error_part = lax.erf(upward * ROOT_HALF)
    activated = (0.5 * upward * (1.0 + error_part)).astype(jnp.bfloat16)
    down_part = jnp.dot(activated, w_down, preferred_element_type=jnp.float32)
    down_total = lax.psum(down_part, "tensor")
    outputs = resid_one + (down_total + b_down)
    grad_b_down = jnp.sum(cotangent, axis=0, dtype=jnp.float32)
    grad_w_down = jnp.einsum("rf,rd->fd", activated, cotangent, preferred_element_type=jnp.float32)
    grad_act = jnp.einsum("rd,fd->rf", cotangent, w_down, preferred_element_type=jnp.float32)
    slope = 0.5 * (1.0 + error_part) + upward * jnp.exp(-0.5 * upward * upward) / ROOT_TWO_PI
    grad_up = (grad_act * slope).astype(jnp.bfloat16)
    grad_w_up = jnp.einsum("rd,rf->df", hidden_two, grad_up, preferred_element_type=jnp.float32)
    grad_b_up = jnp.sum(grad_up, axis=0, dtype=jnp.float32)
    hidden_part = jnp.einsum("rf,df->rd", grad_up, w_up, preferred_element_type=jnp.float32)
    grad_hidden_two = lax.psum(hidden_part, "tensor")
    grad_gain_two = jnp.sum(grad_hidden_two * normed_two, axis=0)
    grad_shift_two = jnp.sum(grad_hidden_two, axis=0)
    grad_resid = cotangent.astype(jnp.float32) + norm_back(
        grad_hidden_two, normed_two, inverse_two, gain_two
    )
    resid_low = grad_resid.astype(jnp.bfloat16)
    grad_b_out = jnp.sum(resid_low, axis=0, dtype=jnp.float32)
    grad_w_out = jnp.einsum(
        "rk,rd->kd", attended_low, resid_low, preferred_element_type=jnp.float32
    )
    grad_attended = jnp.einsum(
        "rd,kd->rk", resid_low, w_out, preferred_element_type=jnp.float32
    ).astype(jnp.bfloat16)
    grad_query, grad_keys, grad_values = lax.map(
        lambda packed: attend_back(*packed),
        (query_seqs, key_seqs, value_seqs, visible, log_norm, grad_attended.reshape(seq_shape)),
    )
    lin_query = rotate_back(
        grad_query.reshape(row_count, head_count, HD) * query_scale, cosine_table, sine_table
    )
    lin_key = rotate_back(grad_keys.reshape(row_count, head_count, HD), cosine_table, sine_table)
    lin_value = grad_values.reshape(row_count, head_count, HD)
    grad_proj = (
        jnp.stack([lin_query, lin_key, lin_value], axis=1)
        .astype(jnp.bfloat16)
        .reshape(row_count, 3 * local_width)
    )
    grad_w_qkv = jnp.einsum(
        "rd,rc->dc", hidden_one, grad_proj, preferred_element_type=jnp.float32
    ).reshape(w_qkv.shape)
    grad_b_qkv = jnp.sum(grad_proj, axis=0, dtype=jnp.float32).reshape(b_qkv.shape)
    input_part = jnp.einsum("rc,dc->rd", grad_proj, flat_qkv, preferred_element_type=jnp.float32)
    grad_hidden_one = lax.psum(input_part, "tensor")
    grad_gain_one = jnp.sum(grad_hidden_one * normed_one, axis=0)
    grad_shift_one = jnp.sum(grad_hidden_one, axis=0)
    grad_inputs = grad_resid + norm_back(grad_hidden_one, normed_one, inverse_one, gain_one)
    summed = lax.psum(
        (
            grad_w_qkv,
            grad_b_qkv,
            grad_w_out,
            grad_b_out,
            grad_gain_one,
            grad_shift_one,
            grad_w_up,
            grad_b_up,
            grad_w_down,
            grad_b_down,
            grad_gain_two,
            grad_shift_two,
        ),
        "dp",
    )
    return (
        outputs.astype(jnp.bfloat16),
        grad_inputs,
        summed[0],
        summed[1],
        summed[2],
        summed[3],
        summed[6],
        summed[7],
        summed[8],
        summed[9],
        summed[4],
        summed[5],
        summed[10],
        summed[11],
    )


def solution(mesh):
    placed = (
        P("dp", None),
        P("dp", None),
        P("dp"),
        P("dp", None),
        P(None, None, "tensor"),
        P(None, "tensor"),
        P("tensor", None),
        P(),
        P(None, "tensor"),
        P("tensor"),
        P("tensor", None),
        P(),
        P(),
        P(),
        P(),
        P(),
    )
    return jax.shard_map(
        per_device,
        mesh=mesh,
        in_specs=placed,
        out_specs=(
            P("dp", None),
            P("dp", None),
            P(None, None, "tensor"),
            P(None, "tensor"),
            P("tensor", None),
            P(),
            P(None, "tensor"),
            P("tensor"),
            P("tensor", None),
            P(),
            P(),
            P(),
            P(),
            P(),
        ),
        check_vma=False,
    )
```

profile of v0, /device:TPU:0, one launch (start us, length us, event | category | flops | bytes accessed | tf_op | source)
XLA Modules:
  0.0 665.6 jit_solution(16734673624633222164)
XLA Ops:
  11.0 3.2 convolution_add_fusion
  18.2 2.5 slice_negate_fusion.2
  29.1 40.3 %while.47 = (s32[]{:T(128)}, bf16[2,512,10,32]{1,3,2,0:T(8,128)(2,1)}, f32[2,10,512]{2,1,0:T(8,128)S(1)}, pred[1024]{0:T(1024)(128)(4,1)S(1)}, bf16[2,512,10,32]...) while((s32[]{:T(128)}, ...), condition=%wide.region_5.6_spmd, body=%wide.region_2.5_spmd.sunk | while | flops 718269440 | bytes 151920272 | solution.py:65
  29.4 3.0 select_reduce_fusion.2
  32.4 4.6 fusion.124
  37.0 2.5 copy-done.3
  39.6 9.8 %fusion.125 = bf16[2,512,10,32]{1,3,2,0:T(8,128)(2,1)} fusion(bf16[2,512,10,32]{1,3,2,0:T(8,128)(2,1)} %get-tuple-element.432, s32[]{:T(128)} %get-tuple-element.431, bf16[1024,10,32]{0,2,1:T(8,128)(2,1)S(1)} %copy-done.16, f32[10,512,1024]{2,1,0:T(8,128)} %copy-done.3, f32[10,512]{1,0:T(8,128)S(1)} %fusion.124, ...), kind=kOutput, calls=%fused_computation.6.clone.1 | convolution fusion | flops 356515840 | bytes 22324736 | tf_op jit(solution)/shard_map/while/body/eval_jaxpr/while/body/eval_jaxpr/hqk,khd->qhd/dot_general | solution.py:60
  49.4 3.0 select_reduce_fusion.2
  52.4 4.6 fusion.124
  59.6 9.8 %fusion.125 = bf16[2,512,10,32]{1,3,2,0:T(8,128)(2,1)} fusion(bf16[2,512,10,32]{1,3,2,0:T(8,128)(2,1)} %get-tuple-element.432, s32[]{:T(128)} %get-tuple-element.431, bf16[1024,10,32]{0,2,1:T(8,128)(2,1)S(1)} %copy-done.16, f32[10,512,1024]{2,1,0:T(8,128)} %copy-done.3, f32[10,512]{1,0:T(8,128)S(1)} %fusion.124, ...), kind=kOutput, calls=%fused_computation.6.clone.1 | convolution fusion | flops 356515840 | bytes 22324736 | tf_op jit(solution)/shard_map/while/body/eval_jaxpr/while/body/eval_jaxpr/hqk,khd->qhd/dot_general | solution.py:60
  74.7 25.0 %all-reduce.8.cloned.1.call-done = f32[1024,640]{1,0:T(8,128)} async-done(((f32[1024,640]{1,0:T(8,128)}), f32[1024,640]{1,0:T(8,128)}) %all-reduce.8.cloned.1.call-update) | async-done | bytes 2621456 | tf_op jit(solution)/shard_map/psum | solution.py:167
  99.7 2.5 fusion.74
  103.1 4.3 multiply_convert_fusion.1
  107.4 4.6 convert_reduce_fusion
  113.5 3.7 fusion.78
  117.8 6.0 fusion.77
  123.7 17.0 %all-reduce.10.cloned.1.call-done = f32[1024,640]{1,0:T(8,128)} async-done(((f32[1024,640]{1,0:T(8,128)}), f32[1024,640]{1,0:T(8,128)}) %all-reduce.10.cloned.1.call-update) | async-done | bytes 2621456 | tf_op jit(solution)/shard_map/psum | solution.py:185
  140.7 4.1 multiply_reduce_fusion.1
  144.9 3.0 convert_reduce_fusion.4
  151.0 3.0 reshape.283
  156.0 144.8 %while.48 = (s32[]{:T(128)}, f32[1024,10,32]{0,2,1:T(8,128)S(1)}, f32[1024,10,32]{0,2,1:T(8,128)}, f32[2,512,10,32]{1,0,3,2:T(2,128)}, bf16[2,512,10,32]{1,3,2,0...) while((s32[]{:T(128)}, f32[1024,10,32]{0,2,1:T(8,128)S(1)}, ...), condition=%wide.region_15.16_spmd.clone, body=%wide.region_13.15_spmd.clone.sunk | while | flops 1741941760 | bytes 224304944 | solution.py:107
  156.0 8.6 %fusion.135 = f32[10,512,1024]{2,1,0:T(8,128)} fusion(bf16[1024,10,32]{0,2,1:T(8,128)(2,1)S(1)} %get-tuple-element.477, bf16[2,512,10,32]{1,3,2,0:T(8,128)(2,1)S(1)} %get-tuple-element.475, s32[]{:T(128)} %get-tuple-element.459), kind=kOutput, calls=%fused_computation.28.clone.1 | convolution fusion | flops 335544320 | bytes 21954564 | tf_op jit(solution)/shard_map/while/body/eval_jaxpr/while/body/eval_jaxpr/qhd,khd->hqk/dot_general | solution.py:82
  164.6 13.6 %multiply_reduce_fusion.7 = (f32[10,512]{1,0:T(8,128)S(1)}, f32[10,512,1024]{2,1,0:T(8,128)}) fusion(f32[10,512,1024]{2,1,0:T(8,128)} %fusion.135, f32[10,512]{1,0:T(8,128)S(1)} %dynamic-slice_bitcast_fusion.2, pred[1024]{0:T(1024)(128)(4,1)S(1)} %get-tuple-element.476, bf16[1024,10,32]{0,2,1:T(8,128)(2,1)S(1)} %copy-done.17, ...), kind=kOutput, calls=%fused_computation.14.clone.1 | convolution fusion | flops 356510720 | bytes 42980356 | tf_op jit(solution)/shard_map/while/body/eval_jaxpr/while/body/eval_jaxpr/qhd,khd->hqk/dot_general | solution.py:87
  178.2 14.2 %multiply_convert_fusion.3 = bf16[10,512,1024]{2,1,0:T(8,128)(2,1)S(1)} fusion(f32[10,512,1024]{2,1,0:T(8,128)} %get-tuple-element.421, f32[10,512,1024]{2,1,0:T(8,128)} %fusion.135, f32[10,512]{1,0:T(8,128)S(1)} %get-tuple-element.422, f32[10,512]{1,0:T(8,128)S(1)} %dynamic-slice_bitcast_fusion.2, pred[1024]{0:T(1024)(128)(4,1)S(1)} %get-tuple-element.476), kind=kLoop, calls=%fused_computation.13.clone.1 | loop fusion | flops 26214400 | bytes 52470784 | tf_op jit(solution)/shard_map/while/body/eval_jaxpr/while/body/eval_jaxpr/convert_element_type | solution.py:91
  192.4 4.1 convolution_bitcast_fusion.3
  196.6 2.6 copy.70
  199.2 12.7 %dynamic_update_slice.31 = f32[2,512,10,32]{1,0,3,2:T(2,128)} dynamic-update-slice(f32[2,512,10,32]{1,0,3,2:T(2,128)} %get-tuple-element.462, f32[1,512,10,32]{1,0,3,2:T(1,128)} %copy.70, s32[]{:T(128)} %get-tuple-element.459, s32[]{:T(128)} %constant.98.clone.1..sunk, s32[]{:T(128)} %constant.98.clone.1..sunk, s32[]{:T(128)} %constant.98.clone.1..sunk) | dynamic-update-slice | bytes 1310724 | tf_op jit(solution)/shard_map/while/body/eval_jaxpr/while/body/jit(dynamic_update_index_in_dim)/dynamic_update_slice | solution.py:65
  211.9 6.0 fusion.136
  218.0 10.2 %fusion.137 = f32[1024,10,32]{0,2,1:T(8,128)} fusion(f32[10,512,1024]{2,1,0:T(8,128)} %fusion.135, f32[10,512]{1,0:T(8,128)S(1)} %dynamic-slice_bitcast_fusion.2, pred[1024]{0:T(1024)(128)(4,1)S(1)} %get-tuple-element.476, f32[1024,10,32]{0,2,1:T(8,128)} %get-tuple-element.461, pred[]{:T(512)S(6)} %compare.3, ...), kind=kOutput, calls=%fused_computation.22.clone.1 | convolution fusion | flops 351928320 | bytes 23954436 | tf_op jit(solution)/shard_map/while/body/eval_jaxpr/while/body/eval_jaxpr/hqk,qhd->khd/dot_general | solution.py:98
  228.2 8.6 %fusion.135 = f32[10,512,1024]{2,1,0:T(8,128)} fusion(bf16[1024,10,32]{0,2,1:T(8,128)(2,1)S(1)} %get-tuple-element.477, bf16[2,512,10,32]{1,3,2,0:T(8,128)(2,1)S(1)} %get-tuple-element.475, s32[]{:T(128)} %get-tuple-element.459), kind=kOutput, calls=%fused_computation.28.clone.1 | convolution fusion | flops 335544320 | bytes 21954564 | tf_op jit(solution)/shard_map/while/body/eval_jaxpr/while/body/eval_jaxpr/qhd,khd->hqk/dot_general | solution.py:82
  236.8 13.6 %multiply_reduce_fusion.7 = (f32[10,512]{1,0:T(8,128)S(1)}, f32[10,512,1024]{2,1,0:T(8,128)}) fusion(f32[10,512,1024]{2,1,0:T(8,128)} %fusion.135, f32[10,512]{1,0:T(8,128)S(1)} %dynamic-slice_bitcast_fusion.2, pred[1024]{0:T(1024)(128)(4,1)S(1)} %get-tuple-element.476, bf16[1024,10,32]{0,2,1:T(8,128)(2,1)S(1)} %copy-done.17, ...), kind=kOutput, calls=%fused_computation.14.clone.1 | convolution fusion | flops 356510720 | bytes 42980356 | tf_op jit(solution)/shard_map/while/body/eval_jaxpr/while/body/eval_jaxpr/qhd,khd->hqk/dot_general | solution.py:87
  250.4 14.2 %multiply_convert_fusion.3 = bf16[10,512,1024]{2,1,0:T(8,128)(2,1)S(1)} fusion(f32[10,512,1024]{2,1,0:T(8,128)} %get-tuple-element.421, f32[10,512,1024]{2,1,0:T(8,128)} %fusion.135, f32[10,512]{1,0:T(8,128)S(1)} %get-tuple-element.422, f32[10,512]{1,0:T(8,128)S(1)} %dynamic-slice_bitcast_fusion.2, pred[1024]{0:T(1024)(128)(4,1)S(1)} %get-tuple-element.476), kind=kLoop, calls=%fused_computation.13.clone.1 | loop fusion | flops 26214400 | bytes 52470784 | tf_op jit(solution)/shard_map/while/body/eval_jaxpr/while/body/eval_jaxpr/convert_element_type | solution.py:91
  264.6 4.1 convolution_bitcast_fusion.3
  268.8 2.6 copy.70
  271.4 12.7 %dynamic_update_slice.31 = f32[2,512,10,32]{1,0,3,2:T(2,128)} dynamic-update-slice(f32[2,512,10,32]{1,0,3,2:T(2,128)} %get-tuple-element.462, f32[1,512,10,32]{1,0,3,2:T(1,128)} %copy.70, s32[]{:T(128)} %get-tuple-element.459, s32[]{:T(128)} %constant.98.clone.1..sunk, s32[]{:T(128)} %constant.98.clone.1..sunk, s32[]{:T(128)} %constant.98.clone.1..sunk) | dynamic-update-slice | bytes 1310724 | tf_op jit(solution)/shard_map/while/body/eval_jaxpr/while/body/jit(dynamic_update_index_in_dim)/dynamic_update_slice | solution.py:65
  284.1 6.0 fusion.136
  290.2 10.6 %fusion.137 = f32[1024,10,32]{0,2,1:T(8,128)} fusion(f32[10,512,1024]{2,1,0:T(8,128)} %fusion.135, f32[10,512]{1,0:T(8,128)S(1)} %dynamic-slice_bitcast_fusion.2, pred[1024]{0:T(1024)(128)(4,1)S(1)} %get-tuple-element.476, f32[1024,10,32]{0,2,1:T(8,128)} %get-tuple-element.461, pred[]{:T(512)S(6)} %compare.3, ...), kind=kOutput, calls=%fused_computation.22.clone.1 | convolution fusion | flops 351928320 | bytes 23954436 | tf_op jit(solution)/shard_map/while/body/eval_jaxpr/while/body/eval_jaxpr/hqk,qhd->khd/dot_general | solution.py:98
  300.7 3.5 reshape.285
  312.7 3.4 fusion.79
  317.5 5.8 fusion.80
  323.4 4.3 fusion.72
  330.2 3.4 fusion.61
  333.7 13.9 %all-reduce.14.cloned.1.call-done = (f32[1024,640]{1,0:T(8,128)}, f32[1024,640]{1,0:T(8,128)}) async-done(((f32[1024,640]{1,0:T(8,128)}, f32[1024,640]{1,0:T(8,128)}), (f32[1024,640]{1,0:T(8,128)}, f32[1024,640]{1,0:T(8,128)})) %all-reduce.14.cloned.1.call-update) | async-done | bytes 5242896 | tf_op jit(solution)/shard_map/psum | solution.py:175
  347.7 2.8 fusion.53
  350.5 81.1 %all-reduce = (f32[3,320]{1,0:T(4,128)}, f32[640]{0:T(1024)}, f32[1280]{0:T(1024)}, f32[640]{0:T(1024)}, f32[640]{0:T(1024)}, /*index=5*/f32[640]{0:T(1024)}, f32[640]{0:T(1024)}, f32[640]{0:T(1024)}) all-reduce(f32[3,320]{1,0:T(4,128)S(1)} %reshape.286, f32[640]{0:T(1024)S(1)} %copy-done.52, ...), channel_id=1, replica_groups=mesh['dp'=16,'tensor'=2] {'dp'}, use_global_device_ids=true, to_apply=%region_21.22 | all-reduce | flops 6080 | bytes 48640 | tf_op jit(solution)/shard_map/psum | solution.py:222
  431.6 4.0 add_convert_fusion
  438.4 211.3 %all-reduce.12.cloned.1.call-done = (f32[640,3,320]{0,2,1:T(8,128)}, f32[320,640]{1,0:T(8,128)}, f32[640,1280]{1,0:T(8,128)}, f32[1280,640]{1,0:T(8,128)}) async-done(((f32[640,3,320]{0,2,1:T(8,128)}, f32[320,640]{1,0:T(8,128)}, f32[640,1280]{1,0:T(8,128)}, f32[1280,640]{1,0:T(8,128)}), (f32[640,3,320]{0,2,1:T(8,128)}, f32[320,640]{1,0:T(8,128)}, f32[640,1280]{1,0:T(8,128)}, ...) | async-done | bytes 9830416 | tf_op jit(solution)/shard_map/psum | solution.py:222
  649.7 3.4 copy.104
  (225 shorter events, 51.8 us)
Async XLA Ops:
  7.2 95.6 %copy-start = (bf16[640,1280]{1,0:T(8,128)(2,1)S(1)}, bf16[640,1280]{1,0:T(8,128)(2,1)}, u32[]{:S(2)}) copy-start(bf16[640,1280]{1,0:T(8,128)(2,1)} %param.28) | copy-start | bytes 4915204
  7.2 92.5 %all-reduce.8.cloned.1.call-start = ((), (), s32[]{:S(2)}) async-start(), calls=%async_computation | async-start | bytes 5242880 | tf_op jit(solution)/shard_map/psum | solution.py:167
  9.0 5.2 copy-start.46
  21.7 4.8 copy-start.63
  32.4 7.1 %copy-start.3 = (f32[10,512,1024]{2,1,0:T(8,128)}, f32[10,512,1024]{2,1,0:T(8,128)S(1)}, u32[]{:S(2)}) copy-start(f32[10,512,1024]{2,1,0:T(8,128)S(1)} %get-tuple-element.409) | copy-start | bytes 62914564 | tf_op jit(solution)/shard_map/while/body/eval_jaxpr/while
  32.4 7.2 %copy-start.16 = (bf16[1024,10,32]{0,2,1:T(8,128)(2,1)S(1)}, bf16[1024,10,32]{0,2,1:T(8,128)(2,1)}, u32[]{:S(2)}) copy-start(bf16[1024,10,32]{0,2,1:T(8,128)(2,1)} %get-tuple-element.445) | copy-start | bytes 1966084 | tf_op jit(solution)/shard_map/while/body/eval_jaxpr/while
  52.4 7.1 %copy-start.3 = (f32[10,512,1024]{2,1,0:T(8,128)}, f32[10,512,1024]{2,1,0:T(8,128)S(1)}, u32[]{:S(2)}) copy-start(f32[10,512,1024]{2,1,0:T(8,128)S(1)} %get-tuple-element.409) | copy-start | bytes 62914564 | tf_op jit(solution)/shard_map/while/body/eval_jaxpr/while
  52.4 7.2 %copy-start.16 = (bf16[1024,10,32]{0,2,1:T(8,128)(2,1)S(1)}, bf16[1024,10,32]{0,2,1:T(8,128)(2,1)}, u32[]{:S(2)}) copy-start(bf16[1024,10,32]{0,2,1:T(8,128)(2,1)} %get-tuple-element.445) | copy-start | bytes 1966084 | tf_op jit(solution)/shard_map/while/body/eval_jaxpr/while
  72.2 27.5 %copy-start.62 = (f32[640]{0:T(1024)S(1)}, f32[640]{0:T(1024)}, u32[]{:S(2)}) copy-start(f32[640]{0:T(1024)} %param.27) | copy-start | bytes 7684
  74.7 66.1 %all-reduce.10.cloned.1.call-start = ((), (), s32[]{:S(2)}) async-start(), calls=%async_computation.1 | async-start | bytes 5242880 | tf_op jit(solution)/shard_map/psum | solution.py:185
  102.2 5.2 copy-start.4
  102.3 42.6 %copy-start.44 = (f32[1024]{0:T(1024)}, f32[1024]{0:T(1024)S(1)}, u32[]{:S(2)}) copy-start(f32[1024]{0:T(1024)S(1)} %broadcast_multiply_fusion.8) | copy-start | bytes 12292
  103.1 41.8 %copy-start.48 = (f32[1024]{0:T(1024)}, f32[1024]{0:T(1024)S(1)}, u32[]{:S(2)}) copy-start(f32[1024]{0:T(1024)S(1)} %add_rsqrt_fusion) | copy-start | bytes 12292
  103.1 4.3 copy-start.35
  103.1 4.3 copy-start.65
  117.2 230.4 %all-reduce.14.cloned.1.call-start = ((), (), s32[]{:S(2)}) async-start(), calls=%async_computation.3 | async-start | bytes 10485760 | tf_op jit(solution)/shard_map/psum | solution.py:175
  140.7 4.1 copy-start.18
  144.9 4.6 copy-start.34
  156.0 8.6 %copy-start.7 = (bf16[2,512,10,32]{1,3,2,0:T(8,128)(2,1)}, bf16[2,512,10,32]{1,3,2,0:T(8,128)(2,1)S(1)}, u32[]{:S(2)}) copy-start(bf16[2,512,10,32]{1,3,2,0:T(8,128)(2,1)S(1)} %get-tuple-element.475) | copy-start | bytes 1966084 | tf_op jit(solution)/shard_map/while/body/eval_jaxpr/while
  156.0 8.6 %copy-start.14 = (bf16[2,512,10,32]{1,3,2,0:T(8,128)(2,1)S(1)}, bf16[2,512,10,32]{1,3,2,0:T(8,128)(2,1)}, u32[]{:S(2)}) copy-start(bf16[2,512,10,32]{1,3,2,0:T(8,128)(2,1)} %get-tuple-element.479) | copy-start | bytes 1966084 | tf_op jit(solution)/shard_map/while/body/eval_jaxpr/while
  156.0 8.6 %copy-start.17 = (bf16[1024,10,32]{0,2,1:T(8,128)(2,1)S(1)}, bf16[1024,10,32]{0,2,1:T(8,128)(2,1)}, u32[]{:S(2)}) copy-start(bf16[1024,10,32]{0,2,1:T(8,128)(2,1)} %get-tuple-element.480) | copy-start | bytes 1966084 | tf_op jit(solution)/shard_map/while/body/eval_jaxpr/while
  211.9 6.0 copy-start.15
  218.0 10.2 %copy-start.8 = (bf16[2,512,10,32]{1,3,2,0:T(8,128)(2,1)S(1)}, bf16[2,512,10,32]{1,3,2,0:T(8,128)(2,1)}, u32[]{:S(2)}) copy-start(bf16[2,512,10,32]{1,3,2,0:T(8,128)(2,1)} %copy-done.7) | copy-start | bytes 1966084 | tf_op jit(solution)/shard_map/while/body/eval_jaxpr/while
  228.2 8.6 %copy-start.7 = (bf16[2,512,10,32]{1,3,2,0:T(8,128)(2,1)}, bf16[2,512,10,32]{1,3,2,0:T(8,128)(2,1)S(1)}, u32[]{:S(2)}) copy-start(bf16[2,512,10,32]{1,3,2,0:T(8,128)(2,1)S(1)} %get-tuple-element.475) | copy-start | bytes 1966084 | tf_op jit(solution)/shard_map/while/body/eval_jaxpr/while
  228.2 8.6 %copy-start.14 = (bf16[2,512,10,32]{1,3,2,0:T(8,128)(2,1)S(1)}, bf16[2,512,10,32]{1,3,2,0:T(8,128)(2,1)}, u32[]{:S(2)}) copy-start(bf16[2,512,10,32]{1,3,2,0:T(8,128)(2,1)} %get-tuple-element.479) | copy-start | bytes 1966084 | tf_op jit(solution)/shard_map/while/body/eval_jaxpr/while
  228.2 8.6 %copy-start.17 = (bf16[1024,10,32]{0,2,1:T(8,128)(2,1)S(1)}, bf16[1024,10,32]{0,2,1:T(8,128)(2,1)}, u32[]{:S(2)}) copy-start(bf16[1024,10,32]{0,2,1:T(8,128)(2,1)} %get-tuple-element.480) | copy-start | bytes 1966084 | tf_op jit(solution)/shard_map/while/body/eval_jaxpr/while
  264.6 4.1 copy-start.2
  284.1 6.0 copy-start.15
  290.2 10.6 %copy-start.8 = (bf16[2,512,10,32]{1,3,2,0:T(8,128)(2,1)S(1)}, bf16[2,512,10,32]{1,3,2,0:T(8,128)(2,1)}, u32[]{:S(2)}) copy-start(bf16[2,512,10,32]{1,3,2,0:T(8,128)(2,1)} %copy-done.7) | copy-start | bytes 1966084 | tf_op jit(solution)/shard_map/while/body/eval_jaxpr/while
  300.7 5.6 copy-start.43
  316.2 7.1 %copy-start.45 = (f32[1024]{0:T(1024)S(1)}, f32[1024]{0:T(1024)}, u32[]{:S(2)}) copy-start(f32[1024]{0:T(1024)} %copy-done.44) | copy-start | bytes 12292
  316.2 7.1 %copy-start.49 = (f32[1024]{0:T(1024)S(1)}, f32[1024]{0:T(1024)}, u32[]{:S(2)}) copy-start(f32[1024]{0:T(1024)} %copy-done.48) | copy-start | bytes 12292
  316.2 7.1 %copy-start.55 = (f32[640]{0:T(1024)S(1)}, f32[640]{0:T(1024)}, u32[]{:S(2)}) copy-start(f32[640]{0:T(1024)} %param.34) | copy-start | bytes 7684
  316.2 7.1 %copy-start.69 = (f32[640]{0:T(1024)S(1)}, f32[640]{0:T(1024)}, u32[]{:S(2)}) copy-start(f32[640]{0:T(1024)} %param.35) | copy-start | bytes 7684
  316.2 333.5 %all-reduce.12.cloned.1.call-start = ((), (), s32[]{:S(2)}) async-start(), calls=%async_computation.2 | async-start | bytes 19660800 | tf_op jit(solution)/shard_map/psum | solution.py:222
  317.5 5.9 copy-start.6
  317.5 5.9 copy-start.73
  323.4 4.3 copy-start.10
  323.4 4.3 copy-start.21
  333.6 16.8 %copy-start.52 = (f32[640]{0:T(1024)S(1)}, f32[640]{0:T(1024)}, u32[]{:S(2)}) copy-start(f32[640]{0:T(1024)} %get-tuple-element.271) | copy-start | bytes 7684
  333.6 16.8 %copy-start.53 = (f32[640]{0:T(1024)S(1)}, f32[640]{0:T(1024)}, u32[]{:S(2)}) copy-start(f32[640]{0:T(1024)} %get-tuple-element.284) | copy-start | bytes 7684
  333.6 16.8 %copy-start.58 = (f32[640]{0:T(1024)S(1)}, f32[640]{0:T(1024)}, u32[]{:S(2)}) copy-start(f32[640]{0:T(1024)} %get-tuple-element.215) | copy-start | bytes 7684
  333.6 16.8 %copy-start.59 = (f32[640]{0:T(1024)S(1)}, f32[640]{0:T(1024)}, u32[]{:S(2)}) copy-start(f32[640]{0:T(1024)} %get-tuple-element.221) | copy-start | bytes 7684
  333.6 16.8 %copy-start.60 = (f32[1280]{0:T(1024)S(1)}, f32[1280]{0:T(1024)}, u32[]{:S(2)}) copy-start(f32[1280]{0:T(1024)} %get-tuple-element.303) | copy-start | bytes 15364
  333.6 98.0 %copy-start.64 = (f32[640]{0:T(1024)S(1)}, f32[640]{0:T(1024)}, u32[]{:S(2)}) copy-start(f32[640]{0:T(1024)} %param.31) | copy-start | bytes 7684
  431.6 4.7 copy-start.19
  649.7 4.3 copy-start.28
  654.0 4.8 copy-start.1
  (38 other events, 93.1 us)
Sparse Core Ops, SparseCore 0:
  74.8 24.8 all-reduce.7
  117.3 23.3 all-reduce.9
  316.3 31.3 all-reduce.13
  356.2 293.4 all-reduce.11
where the time goes:
time: 673 us; the launch traced here: 666 us
  waiting for transfers between devices  267 us (40%)
  matrix products  156 us (23%)
  blocking collectives  81.1 us (12%)
  local copies, waits for them, and re-layouts  74.2 us (11%)
  other arithmetic  71 us (11%)
  between operations  15.3 us (2%)
    psum x1, waiting for transfers between devices, per_device(): lax.psum((grad_w_qkv, grad_b_qkv, grad_w_out, grad_b_out, grad_gain_one,...  211 us
    psum x1, blocking collectives, per_device(): lax.psum((grad_w_qkv, grad_b_qkv, grad_w_out, grad_b_out, grad_gain_one,...  81.1 us
    dynamic_update_slice x4, local copies, waits for them, and re-layouts, attend_sequence(): attended, log_norm = lax.map(one_block, query_blocks)  30.7 us
    convert_element_type x2, other arithmetic, one_block(): grad_scores = (chances * (grad_chances - inner)).astype(jnp.bfloat16)  28.4 us
    dot_general x2, matrix products, one_block(): jnp.einsum('qhd,khd->hqk', grad_block, value_rows, preferred_element_type...  27.2 us
    psum x1, waiting for transfers between devices, per_device(): mix_total = lax.psum(mix_part, 'tensor')  25 us
    dot_general x4, matrix products, one_block(): jnp.einsum('qhd,khd->hqk', query_block, key_rows, preferred_element_type=...  23.2 us
    unnamed x138, local copies, waits for them, and re-layouts  20.8 us
  transfers between devices with their start and end apart: 4, of which 4 were waited for; matrix products, arithmetic and copies ran while one was open for 5% of the time, Pallas kernels for 0%

commit v1 on v0

v1 whole, which is shorter than its diff:
```python
import functools
import math

import jax
import jax.numpy as jnp
import numpy as np
from jax import lax
from jax.experimental import pallas as pl
from jax.experimental.pallas import tpu as pltpu
from jax.sharding import PartitionSpec as P

HD = 32
HALF = HD // 2
EPSILON = 1e-05
ROOT_HALF = 0.7071067811865476
ROOT_TWO_PI = 2.5066282746310002
LOG2E = math.log2(math.e)
HIDDEN_BIAS = -1e30
SAFE_POWER = 96.0
f32 = jnp.float32
bf16 = jnp.bfloat16


def dot_nn(a, b):
    return lax.dot_general(a, b, (((1,), (0,)), ((), ())), preferred_element_type=f32)


def dot_nt(a, b):
    return lax.dot_general(a, b, (((1,), (1,)), ((), ())), preferred_element_type=f32)


def dot_tn(a, b):
    return lax.dot_general(a, b, (((0,), (0,)), ((), ())), preferred_element_type=f32)


def normalize(values):
    centre = jnp.mean(values, axis=1, keepdims=True)
    shifted = values - centre
    inverse = lax.rsqrt(jnp.mean(shifted * shifted, axis=1, keepdims=True) + EPSILON)
    return shifted * inverse, inverse


def norm_back(grad_normed, normed, inverse, gain_vec):
    scaled = grad_normed * gain_vec
    first_mean = jnp.mean(scaled, axis=1, keepdims=True)
    second_mean = jnp.mean(scaled * normed, axis=1, keepdims=True)
    return inverse * (scaled - first_mean - normed * second_mean)


def split_three(values):
    first = values.astype(bf16)
    rest = values - first.astype(f32)
    second = rest.astype(bf16)
    third = (rest - second.astype(f32)).astype(bf16)
    return first, second, third


def stack_rows(*rows):
    count = rows[0].shape[1]
    place = lax.broadcasted_iota(jnp.int32, (16, count), 0)
    out = jnp.zeros((16, count), f32)
    for index, row in enumerate(rows):
        out = jnp.where(place == index, row, out)
    return out.astype(bf16)


def rope_rows(values, cosine, sine):
    heads = values.reshape(-1, 2, HALF, values.shape[1])
    lower, upper = heads[:, 0], heads[:, 1]
    turned = jnp.stack([lower * cosine - upper * sine, upper * cosine + lower * sine], axis=1)
    return turned.reshape(values.shape)


def rope_back_rows(values, cosine, sine):
    heads = values.reshape(-1, 2, HALF, values.shape[1])
    lower, upper = heads[:, 0], heads[:, 1]
    turned = jnp.stack([lower * cosine + upper * sine, upper * cosine - lower * sine], axis=1)
    return turned.reshape(values.shape)


def spread_chunks(total_ref, keep_ref, send_ref, me, count):
    size = total_ref.shape[0] // count
    half = count // 2
    for place in range(count):
        chunk = jnp.bitwise_xor(me, place)
        rows = total_ref[pl.ds(pl.multiple_of(chunk * size, size), size), :]
        target = keep_ref if place < half else send_ref
        start = (place % half) * size
        target[start : start + size, :] = rows


def front_kernel(
    block,
    steps,
    length_ref,
    tokens_ref,
    w_ref,
    b_ref,
    gain_ref,
    shift_ref,
    cos_ref,
    sin_ref,
    mask_ref,
    w_out_ref,
    hidden_ref,
    q_ref,
    k_ref,
    v_ref,
    att_ref,
    lse_ref,
    bias_ref,
    mix_ref,
):
    step = pl.program_id(0)
    seq_len = q_ref.shape[1]
    width = q_ref.shape[0]
    per_step = 2
    query_scale = HD ** (-0.5)

    @pl.when(step == 0)
    def _():
        place = lax.broadcasted_iota(jnp.int32, (1, seq_len), 1)
        visible = (place < length_ref[0]) & (mask_ref[...] == 1) | (place == 0)
        bias_ref[...] = jnp.where(visible, 0.0, HIDDEN_BIAS)

    @pl.when(step < steps)
    def _():
        normed, _ = normalize(tokens_ref[...].astype(f32))
        hidden = (normed * gain_ref[...] + shift_ref[...]).astype(bf16)
        hidden_ref[...] = hidden
        projected = dot_nt(w_ref[...].reshape(3 * width, w_ref.shape[2]), hidden)
        columns = pl.ds(pl.multiple_of(step * block, block), block)
        parts = []
        for index in range(3):
            column = jnp.broadcast_to(b_ref[index : index + 1, :], (128, width)).T
            column = jnp.concatenate([column] * (block // 128), axis=1)
            parts.append(projected[index * width : (index + 1) * width] + column)
        cosine, sine = cos_ref[...], sin_ref[...]
        q_ref[:, columns] = (rope_rows(parts[0], cosine, sine) * query_scale).astype(bf16)
        k_ref[:, columns] = rope_rows(parts[1], cosine, sine).astype(bf16)
        v_ref[:, columns] = parts[2].astype(bf16)

    @pl.when(step >= steps)
    def _():
        ones = jnp.ones((1, seq_len), f32)
        key_extra = stack_rows(bias_ref[...])
        value_extra = stack_rows(ones)
        query_extra = stack_rows(ones)
        first_head = (step - steps) * per_step
        queries, keys, values, bounds = [], [], [], []
        for index in range(per_step):
            rows = pl.ds(pl.multiple_of((first_head + index) * HD, HD), HD)
            key = k_ref[rows, :]
            query = q_ref[rows, :].astype(f32) * LOG2E
            key_wide = key.astype(f32)
            bounds.append(
                jnp.max(jnp.sum(query * query, axis=0, keepdims=True))
                * jnp.max(jnp.sum(key_wide * key_wide, axis=0, keepdims=True))
            )
            queries.append(jnp.concatenate([*split_three(query), query_extra], axis=0))
            keys.append(jnp.concatenate([key, key, key, key_extra], axis=0))
            values.append(jnp.concatenate([v_ref[rows, :], value_extra], axis=0))
        bound = bounds[0]
        for other in bounds[1:]:
            bound = jnp.maximum(bound, other)

        def attend(shifted):
            size = min(512, seq_len)
            for index in range(per_step):
                head = first_head + index
                rows = pl.ds(pl.multiple_of(head * HD, HD), HD)
                for start in range(0, seq_len, size):
                    part = slice(start, start + size)
                    scores = dot_tn(keys[index], queries[index][:, part])
                    if shifted:
                        peak = jnp.max(scores, axis=0, keepdims=True)
                        powers = jnp.exp2(scores - peak)
                    else:
                        peak = 0.0
                        powers = jnp.exp2(scores)
                    summed = dot_nn(values[index], powers.astype(bf16))
                    total = summed[HD : HD + 1, :]
                    att_ref[rows, part] = (summed[:HD] * (1.0 / total)).astype(bf16)
                    lse_ref[head, :, part] = peak + jnp.log(total) * LOG2E

        small = bound < SAFE_POWER * SAFE_POWER

        @pl.when(small)
        def _():
            attend(False)

        @pl.when(jnp.logical_not(small))
        def _():
            attend(True)

    @pl.when(step == pl.num_programs(0) - 1)
    def _():
        mix_ref[...] = dot_tn(att_ref[...], w_out_ref[...])


def const_spec(shape, index=None):
    where = tuple(index) if index is not None else (0,) * len(shape)
    return pl.BlockSpec(shape, lambda *_: where, pipeline_mode=pl.Buffered(1))


def out_spec(shape):
    where = (0,) * len(shape)
    return pl.BlockSpec(shape, lambda *_: where)


def front(tokens, lengths, pad_mask, w_t, b_qkv, w_out, gain_one, shift_one, cosine, sine):
    rows, model = tokens.shape
    width = w_t.shape[1]
    heads = width // HD
    block = min(256, rows)
    steps = rows // block
    clipped = lambda i: (jnp.minimum(i, steps - 1), 0)
    clipped_lanes = lambda i: (0, jnp.minimum(i, steps - 1))
    return pl.pallas_call(
        functools.partial(front_kernel, block, steps),
        grid=(steps + heads // 2,),
        in_specs=[
            pl.BlockSpec(memory_space=pltpu.SMEM),
            pl.BlockSpec((block, model), clipped),
            const_spec(w_t.shape),
            const_spec(b_qkv.shape),
            const_spec((1, model)),
            const_spec((1, model)),
            pl.BlockSpec((HALF, block), clipped_lanes),
            pl.BlockSpec((HALF, block), clipped_lanes),
            const_spec(pad_mask.shape),
            const_spec(w_out.shape),
        ],
        out_specs=[
            pl.BlockSpec((block, model), clipped),
            out_spec((width, rows)),
            out_spec((width, rows)),
            out_spec((width, rows)),
            out_spec((width, rows)),
            out_spec((heads, 1, rows)),
            out_spec((1, rows)),
            out_spec((rows, model)),
        ],
        out_shape=[
            jax.ShapeDtypeStruct((rows, model), bf16),
            jax.ShapeDtypeStruct((width, rows), bf16),
            jax.ShapeDtypeStruct((width, rows), bf16),
            jax.ShapeDtypeStruct((width, rows), bf16),
            jax.ShapeDtypeStruct((width, rows), bf16),
            jax.ShapeDtypeStruct((heads, 1, rows), f32),
            jax.ShapeDtypeStruct((1, rows), f32),
            jax.ShapeDtypeStruct((rows, model), f32),
        ],
        compiler_params=pltpu.CompilerParams(vmem_limit_bytes=32 << 20),
        cost_estimate=pl.CostEstimate(
            flops=20 * 10**9, bytes_accessed=10 << 20, transcendentals=10 << 20
        ),
        name="front",
    )(lengths, tokens, w_t, b_qkv, gain_one, shift_one, cosine, sine, pad_mask, w_out)


def mlp_kernel(first, count, *refs):
    if first:
        (me_ref, tokens_ref, own_ref, other_ref, b_out_ref, gain_ref, shift_ref) = refs[:7]
        refs = refs[7:]
    else:
        (me_ref, hidden_ref, down_in_ref, hid_in_ref) = refs[:4]
        refs = refs[4:]
    cot_ref, w_up_ref, b_up_ref, w_down_ref = refs[:4]
    refs = refs[4:]
    if first:
        resid_ref, hidden_ref = refs[:2]
        refs = refs[2:]
    (down_ref, hid_ref, wd_keep, wd_send, wu_keep, wu_send, b_up_sum, wd_total, wu_total) = refs[:9]
    step = pl.program_id(0)

    @pl.when(step == 0)
    def _():
        wd_total[...] = jnp.zeros_like(wd_total)
        wu_total[...] = jnp.zeros_like(wu_total)
        b_up_sum[...] = jnp.zeros_like(b_up_sum)

    if first:
        resid = tokens_ref[...].astype(f32) + ((own_ref[...] + other_ref[...]) + b_out_ref[...])
        resid_ref[...] = resid
        normed, _ = normalize(resid)
        hidden = (normed * gain_ref[...] + shift_ref[...]).astype(bf16)
        hidden_ref[...] = hidden
    else:
        hidden = hidden_ref[...]
    cot = cot_ref[...]
    w_up, w_down = w_up_ref[...], w_down_ref[...]
    upward = dot_nn(hidden, w_up) + b_up_ref[...]
    error_part = lax.erf(upward * ROOT_HALF)
    activated = (0.5 * upward * (1.0 + error_part)).astype(bf16)
    wd_total[...] += dot_tn(activated, cot)
    grad_act = dot_nt(cot, w_down)
    slope = 0.5 * (1.0 + error_part) + upward * jnp.exp(-0.5 * upward * upward) / ROOT_TWO_PI
    grad_up = (grad_act * slope).astype(bf16)
    wu_total[...] += dot_tn(hidden, grad_up)
    b_up_sum[...] += jnp.sum(grad_up.astype(f32), axis=0, keepdims=True)
    down = dot_nn(activated, w_down)
    hid = dot_nt(grad_up, w_up)
    if not first:
        down = down + down_in_ref[...]
        hid = hid + hid_in_ref[...]
    down_ref[...] = down
    hid_ref[...] = hid

    @pl.when(step == pl.num_programs(0) - 1)
    def _():
        spread_chunks(wd_total, wd_keep, wd_send, me_ref[0], count)
        spread_chunks(wu_total, wu_keep, wu_send, me_ref[1], count)


def mlp(first, half, count, me, extras, cotangent, w_up, b_up, w_down):
    rows, model = cotangent.shape
    hidden_half = w_up.shape[1] // 2
    block = min(256, rows)
    row_spec = pl.BlockSpec((block, model), lambda i: (i, 0))
    vec_spec = const_spec((1, model))
    in_specs = [pl.BlockSpec(memory_space=pltpu.SMEM)]
    in_specs += [row_spec] * 3 + ([vec_spec] * 3 if first else [])
    in_specs += [
        row_spec,
        const_spec((model, hidden_half), (0, half)),
        const_spec((1, hidden_half), (0, half)),
        const_spec((hidden_half, model), (half, 0)),
    ]
    rows_f32 = jax.ShapeDtypeStruct((rows, model), f32)
    rows_b16 = jax.ShapeDtypeStruct((rows, model), bf16)
    down_half = jax.ShapeDtypeStruct((hidden_half // 2, model), f32)
    up_half = jax.ShapeDtypeStruct((model // 2, hidden_half), f32)
    out_shape = ([rows_f32, rows_b16] if first else []) + [rows_f32, rows_f32]
    out_specs = [row_spec] * len(out_shape)
    out_shape += [down_half, down_half, up_half, up_half]
    out_shape += [jax.ShapeDtypeStruct((1, hidden_half), f32)]
    out_specs += [out_spec(s.shape) for s in out_shape[len(out_specs) :]]
    return pl.pallas_call(
        functools.partial(mlp_kernel, first, count),
        grid=(rows // block,),
        in_specs=in_specs,
        out_specs=out_specs,
        out_shape=out_shape,
        scratch_shapes=[
            pltpu.VMEM((hidden_half, model), f32),
            pltpu.VMEM((model, hidden_half), f32),
        ],
        compiler_params=pltpu.CompilerParams(vmem_limit_bytes=40 << 20),
        cost_estimate=pl.CostEstimate(
            flops=6 * 2 * rows * model * hidden_half,
            bytes_accessed=20 << 20,
            transcendentals=2 * rows * hidden_half,
        ),
        name="mlp_a" if first else "mlp_b",
    )(me, *extras, cotangent, w_up, b_up, w_down)


def middle_kernel(
    resid_ref,
    own_ref,
    other_ref,
    cot_ref,
    gain_ref,
    w_out_ref,
    grad_resid_ref,
    low_ref,
    grad_att_ref,
    sums_ref,
):
    step = pl.program_id(0)

    @pl.when(step == 0)
    def _():
        sums_ref[...] = jnp.zeros_like(sums_ref)

    normed, inverse = normalize(resid_ref[...])
    grad_hidden = own_ref[...] + other_ref[...]
    cot = cot_ref[...].astype(f32)
    grad_resid = cot + norm_back(grad_hidden, normed, inverse, gain_ref[...])
    low = grad_resid.astype(bf16)
    grad_resid_ref[...] = grad_resid
    low_ref[...] = low
    grad_att_ref[...] = dot_nt(w_out_ref[...], low).astype(bf16)
    sums_ref[0:1, :] += jnp.sum(grad_hidden * normed, axis=0, keepdims=True)
    sums_ref[1:2, :] += jnp.sum(grad_hidden, axis=0, keepdims=True)
    sums_ref[2:3, :] += jnp.sum(low.astype(f32), axis=0, keepdims=True)
    sums_ref[3:4, :] += jnp.sum(cot, axis=0, keepdims=True)


def middle(resid, own, other, cotangent, gain_two, w_out):
    rows, model = resid.shape
    width = w_out.shape[0]
    block = min(256, rows)
    row_spec = pl.BlockSpec((block, model), lambda i: (i, 0))
    return pl.pallas_call(
        middle_kernel,
        grid=(rows // block,),
        in_specs=[row_spec] * 4 + [const_spec((1, model)), const_spec(w_out.shape)],
        out_specs=[
            row_spec,
            row_spec,
            pl.BlockSpec((width, block), lambda i: (0, i)),
            out_spec((8, model)),
        ],
        out_shape=[
            jax.ShapeDtypeStruct((rows, model), f32),
            jax.ShapeDtypeStruct((rows, model), bf16),
            jax.ShapeDtypeStruct((width, rows), bf16),
            jax.ShapeDtypeStruct((8, model), f32),
        ],
        compiler_params=pltpu.CompilerParams(vmem_limit_bytes=24 << 20),
        cost_estimate=pl.CostEstimate(
            flops=2 * rows * model * width, bytes_accessed=12 << 20, transcendentals=rows
        ),
        name="middle",
    )(resid, own, other, cotangent, gain_two, w_out)


def attend_back_kernel(first, count, *refs):
    (
        me_ref,
        q_ref,
        k_ref,
        v_ref,
        att_ref,
        grad_att_ref,
        lse_ref,
        bias_ref,
        cos_ref,
        sin_ref,
        w_ref,
        hidden_ref,
        low_ref,
    ) = refs[:13]
    refs = refs[13:]
    if not first:
        part_in_ref = refs[0]
        refs = refs[1:]
    keep_ref, send_ref, part_ref, b_ref, grad_sc, total_sc = refs
    step = pl.program_id(0)
    seq_len = q_ref.shape[1]
    width = q_ref.shape[0]
    query_scale = HD ** (-0.5)
    rows = pl.ds(pl.multiple_of(step * HD, HD), HD)
    ones = jnp.ones((1, seq_len), f32)
    key, value, query_all = k_ref[rows, :], v_ref[rows, :], q_ref[rows, :]
    keys = jnp.concatenate([key, key, key, stack_rows(bias_ref[...], ones, ones, ones)], axis=0)
    values = jnp.concatenate([value, stack_rows(ones, ones, ones)], axis=0)
    cosine, sine = cos_ref[...], sin_ref[...]
    grad_all = grad_att_ref[rows, :]
    log_all = -lse_ref[step]
    inner_all = -jnp.sum(
        grad_all.astype(f32) * att_ref[rows, :].astype(f32), axis=0, keepdims=True
    )
    grad_key = jnp.zeros((HD, seq_len), f32)
    grad_value = jnp.zeros((HD, seq_len), f32)
    grad_query = []
    size = min(512, seq_len)
    for start in range(0, seq_len, size):
        part = slice(start, start + size)
        query = query_all[:, part]
        logs = [piece.astype(f32) for piece in split_three(log_all[:, part])]
        queries = jnp.concatenate(
            [
                *split_three(query.astype(f32) * LOG2E),
                stack_rows(ones[:, :size], *logs),
            ],
            axis=0,
        )
        chances = jnp.exp2(dot_tn(keys, queries))
        grad_out = grad_all[:, part]
        inner = [piece.astype(f32) for piece in split_three(inner_all[:, part])]
        grads = jnp.concatenate([grad_out, stack_rows(*inner)], axis=0)
        grad_scores = (chances * dot_tn(values, grads)).astype(bf16)
        grad_value = grad_value + dot_nt(grad_out, chances.astype(bf16))
        grad_key = grad_key + dot_nt(query, grad_scores)
        grad_query.append(dot_nn(key, grad_scores))
    grad_query = jnp.concatenate(grad_query, axis=1) * query_scale
    grad_sc[0, rows, :] = rope_back_rows(grad_query, cosine, sine).astype(bf16)
    grad_sc[1, rows, :] = rope_back_rows(grad_key, cosine, sine).astype(bf16)
    grad_sc[2, rows, :] = grad_value.astype(bf16)

    @pl.when(step == pl.num_programs(0) - 1)
    def _():
        grads = grad_sc[...].reshape(3 * width, seq_len)
        total_sc[: 3 * width, :] = dot_nn(grads, hidden_ref[...])
        total_sc[3 * width :, :] = dot_nn(att_ref[...], low_ref[...])
        spread_chunks(total_sc, keep_ref, send_ref, me_ref[0], count)
        weights = w_ref[...].reshape(3 * width, w_ref.shape[2])
        part = dot_tn(grads, weights)
        if not first:
            part = part + part_in_ref[...]
        part_ref[...] = part
        b_ref[...] = dot_nt(jnp.ones((8, seq_len), bf16), grads)


def attend_back(first, half, count, me, rows_in, lse, bias, cosine, sine, w_t, hidden, low, part):
    width, rows = rows_in[0].shape
    width //= 2
    model = hidden.shape[1]
    heads = width // HD
    head_spec = const_spec((width, rows), (half, 0))
    in_specs = [pl.BlockSpec(memory_space=pltpu.SMEM)] + [head_spec] * 5
    in_specs += [
        const_spec((heads, 1, rows), (half, 0, 0)),
        const_spec((1, rows)),
        const_spec((HALF, rows)),
        const_spec((HALF, rows)),
        const_spec((3, width, model), (0, half, 0)),
        const_spec((rows, model)),
        const_spec((rows, model)),
    ]
    extra = []
    if not first:
        in_specs.append(const_spec((rows, model)))
        extra = [part]
    pack = jax.ShapeDtypeStruct((2 * width, model), f32)
    out_shape = [
        pack,
        pack,
        jax.ShapeDtypeStruct((rows, model), f32),
        jax.ShapeDtypeStruct((8, 3 * width), f32),
    ]
    return pl.pallas_call(
        functools.partial(attend_back_kernel, first, count),
        grid=(heads,),
        in_specs=in_specs,
        out_specs=[out_spec(s.shape) for s in out_shape],
        out_shape=out_shape,
        scratch_shapes=[
            pltpu.VMEM((3, width, rows), bf16),
            pltpu.VMEM((4 * width, model), f32),
        ],
        compiler_params=pltpu.CompilerParams(vmem_limit_bytes=40 << 20),
        cost_estimate=pl.CostEstimate(
            flops=14 * 10**9, bytes_accessed=10 << 20, transcendentals=5 << 20
        ),
        name="attend_back_a" if first else "attend_back_b",
    )(me, *rows_in, lse, bias, cosine, sine, w_t, hidden, low, *extra)


def last_kernel(tokens_ref, own_ref, other_ref, grad_resid_ref, gain_ref, grad_ref, sums_ref):
    step = pl.program_id(0)

    @pl.when(step == 0)
    def _():
        sums_ref[...] = jnp.zeros_like(sums_ref)

    normed, inverse = normalize(tokens_ref[...].astype(f32))
    grad_hidden = own_ref[...] + other_ref[...]
    grad_ref[...] = grad_resid_ref[...] + norm_back(grad_hidden, normed, inverse, gain_ref[...])
    sums_ref[0:1, :] += jnp.sum(grad_hidden * normed, axis=0, keepdims=True)
    sums_ref[1:2, :] += jnp.sum(grad_hidden, axis=0, keepdims=True)


def last(tokens, own, other, grad_resid, gain_one):
    rows, model = tokens.shape
    block = min(256, rows)
    row_spec = pl.BlockSpec((block, model), lambda i: (i, 0))
    return pl.pallas_call(
        last_kernel,
        grid=(rows // block,),
        in_specs=[row_spec] * 4 + [const_spec((1, model))],
        out_specs=[row_spec, out_spec((8, model))],
        out_shape=[
            jax.ShapeDtypeStruct((rows, model), f32),
            jax.ShapeDtypeStruct((8, model), f32),
        ],
        compiler_params=pltpu.CompilerParams(vmem_limit_bytes=24 << 20),
        cost_estimate=pl.CostEstimate(
            flops=20 * rows * model, bytes_accessed=12 << 20, transcendentals=rows
        ),
        name="last",
    )(tokens, own, other, grad_resid, gain_one)


def flip(values, bit, size):
    return lax.ppermute(values, "dp", [(i, i ^ (1 << bit)) for i in range(size)])


class Chain:
    def __init__(self, order, size, keep, send):
        self.order, self.size = order, size
        self.keep, self.send = keep, send

    def reduce(self):
        keep, send = self.keep, self.send
        for index, bit in enumerate(self.order):
            total = keep + flip(send, bit, self.size)
            if index + 1 < len(self.order):
                half = total.shape[0] // 2
                keep, send = total[:half], total[half:]
        for bit in range(len(self.order), self.size.bit_length() - 1):
            total = total + flip(total, bit, self.size)
        self.own = total

    def gather(self):
        own = self.own
        for bit in self.order[:0:-1]:
            own = jnp.concatenate([own, flip(own, bit, self.size)], axis=0)
        return own, flip(own, self.order[0], self.size)


def place_index(order):
    index = lax.axis_index("dp")
    out = jnp.zeros((), jnp.int32)
    for bit in order:
        out = out * 2 + jnp.bitwise_and(jnp.right_shift(index, bit), 1)
    return out


def assemble_kernel(kind, count, me_ref, *refs):
    pieces, rest = refs[:4], refs[4:]
    outs, sem = rest[:-1], rest[-1]
    half = count // 2
    size = pieces[0].shape[0] // half
    for wait in (False, True):
        for group in range(2):
            for place in range(count):
                chunk = jnp.bitwise_xor(me_ref[group], place)
                source = pieces[2 * group + place // half].at[
                    pl.ds((place % half) * size, size), :
                ]
                slot = sem.at[group * count + place]
                row = pl.multiple_of(chunk * size, size)

                def move(target):
                    copy = pltpu.make_async_copy(source, target, slot)
                    copy.wait() if wait else copy.start()

                if kind == "down":
                    total = outs[0].shape[0] // 2
                    move(outs[0].at[pl.ds(pl.multiple_of(group * total + row, size), size), :])
                elif kind == "up":
                    total = outs[0].shape[1] // 2
                    move(outs[0].at[pl.ds(row, size), pl.ds(group * total, total)])
                else:
                    width = outs[1].shape[0] // 2
                    per = width // size
                    quarter = chunk // per
                    inside = (chunk - quarter * per) * size
                    inner = pl.multiple_of(group * width + inside, size)

                    @pl.when(quarter < 3)
                    def _():
                        where = pl.multiple_of(quarter * 2 * width + inner, size)
                        move(outs[0].at[pl.ds(where, size), :])

                    @pl.when(quarter >= 3)
                    def _():
                        move(outs[1].at[pl.ds(inner, size), :])


def assemble(kind, count, me, pieces, shapes):
    anywhere = pl.BlockSpec(memory_space=pl.ANY)
    return pl.pallas_call(
        functools.partial(assemble_kernel, kind, count),
        in_specs=[pl.BlockSpec(memory_space=pltpu.SMEM)] + [anywhere] * 4,
        out_specs=[anywhere] * len(shapes),
        out_shape=[jax.ShapeDtypeStruct(shape, f32) for shape in shapes],
        scratch_shapes=[pltpu.SemaphoreType.DMA((2 * count,))],
        compiler_params=pltpu.CompilerParams(vmem_limit_bytes=2 << 20),
        cost_estimate=pl.CostEstimate(flops=0, bytes_accessed=7 << 20, transcendentals=0),
        name="assemble_" + kind,
    )(me, *pieces)


def per_device(
    size,
    tokens,
    cotangent,
    lengths,
    pad_mask,
    w_qkv,
    b_qkv,
    w_out,
    b_out,
    w_up,
    b_up,
    w_down,
    b_down,
    gain_one,
    shift_one,
    gain_two,
    shift_two,
):
    rows, model = tokens.shape
    width = w_qkv.shape[2]
    hidden = w_up.shape[1]
    count = min(16, size)
    bits = count.bit_length() - 1
    order_a = list(range(bits))
    order_b = order_a[:2][::-1] + order_a[2:]
    me_a, me_b = place_index(order_a), place_index(order_b)
    me = {0: me_a, 1: me_b}
    orders = {0: order_a, 1: order_b}

    frequency = np.float32(10000.0) ** (
        -(np.float32(2.0) * np.arange(HALF, dtype=np.float32)) / np.float32(HD)
    )
    angles = frequency.astype(np.float32)[:, None] * np.arange(rows, dtype=np.float32)[None, :]
    cosine = jnp.asarray(np.cos(angles.astype(np.float32)), f32)
    sine = jnp.asarray(np.sin(angles.astype(np.float32)), f32)
    row_of = lambda vec: vec.reshape(1, -1)
    swap = lambda values: lax.ppermute(values, "tensor", [(0, 1), (1, 0)])
    w_t = jnp.transpose(w_qkv, (1, 2, 0))

    hidden_one, q, k, v, att, lse, bias, mix = front(
        tokens,
        lengths,
        pad_mask,
        w_t,
        b_qkv,
        w_out,
        row_of(gain_one),
        row_of(shift_one),
        cosine,
        sine,
    )
    mix_other = swap(mix)
    me_ab = jnp.stack([me_a, me_b])
    me_ba = jnp.stack([me_b, me_a])
    resid, hidden_two, down, hid, d1k, d1s, u1k, u1s, gb_up1 = mlp(
        True,
        0,
        count,
        me_ab,
        (tokens, mix, mix_other, row_of(b_out), row_of(gain_two), row_of(shift_two)),
        cotangent,
        w_up,
        row_of(b_up),
        w_down,
    )
    down, hid, d2k, d2s, u2k, u2s, gb_up2 = mlp(
        False,
        1,
        count,
        me_ba,
        (hidden_two, down, hid),
        cotangent,
        w_up,
        row_of(b_up),
        w_down,
    )
    d1 = Chain(order_a, size, d1k, d1s)
    u1 = Chain(order_b, size, u1k, u1s)
    d2 = Chain(order_b, size, d2k, d2s)
    u2 = Chain(order_a, size, u2k, u2s)
    hid_other = swap(hid)
    grad_resid, low, grad_att, sums_two = middle(
        resid, hid, hid_other, cotangent, row_of(gain_two), w_out
    )
    down_other = swap(down)
    outputs = (resid + ((down + down_other) + b_down)).astype(bf16)
    rows_in = (q, k, v, att, grad_att)
    q1k, q1s, part, gb1 = attend_back(
        True, 0, count, me_ab[:1], rows_in, lse, bias, cosine, sine, w_t, hidden_one, low, None
    )
    q1 = Chain(order_a, size, q1k, q1s)
    q2k, q2s, part, gb2 = attend_back(
        False, 1, count, me_ba[:1], rows_in, lse, bias, cosine, sine, w_t, hidden_one, low, part
    )
    q2 = Chain(order_b, size, q2k, q2s)
    part_other = swap(part)
    grad_tokens, sums_one = last(tokens, part, part_other, grad_resid, row_of(gain_one))

    pad = model - 3 * width // 2
    small = jnp.concatenate(
        [
            sums_one[:2],
            sums_two[:4],
            jnp.pad(gb1[:1], ((0, 0), (0, pad))),
            jnp.pad(gb2[:1], ((0, 0), (0, pad))),
            gb_up1.reshape(-1, model),
            gb_up2.reshape(-1, model),
        ],
        axis=0,
    )
    for bit in range(size.bit_length() - 1):
        small = small + flip(small, bit, size)

    chains = [d1, u1, d2, u2, q1, q2]
    for chain in chains:
        chain.reduce()
    done = [chain.gather() for chain in chains]
    (grad_w_down,) = assemble("down", count, me_ab, done[0] + done[2], [(hidden, model)])
    (grad_w_up,) = assemble("up", count, me_ba, done[1] + done[3], [(model, hidden)])
    grad_w_qkv, grad_w_out = assemble(
        "attention", count, me_ab, done[4] + done[5], [(3 * width, model), (width, model)]
    )
    grad_w_qkv = jnp.transpose(grad_w_qkv.reshape(3, width, model), (2, 0, 1))
    grad_b_qkv = small[6:8, : 3 * width // 2].reshape(2, 3, width // 2)
    grad_b_qkv = jnp.transpose(grad_b_qkv, (1, 0, 2)).reshape(3, width)
    return (
        outputs,
        grad_tokens,
        grad_w_qkv,
        grad_b_qkv,
        grad_w_out,
        small[4],
        grad_w_up,
        small[8:].reshape(-1),
        grad_w_down,
        small[5],
        small[0],
        small[1],
        small[2],
        small[3],
    )


def solution(mesh):
    placed = (
        P("dp", None),
        P("dp", None),
        P("dp"),
        P("dp", None),
        P(None, None, "tensor"),
        P(None, "tensor"),
        P("tensor", None),
        P(),
        P(None, "tensor"),
        P("tensor"),
        P("tensor", None),
        P(),
        P(),
        P(),
        P(),
        P(),
    )
    return jax.shard_map(
        functools.partial(per_device, mesh.shape["dp"]),
        mesh=mesh,
        in_specs=placed,
        out_specs=(
            P("dp", None),
            P("dp", None),
            P(None, None, "tensor"),
            P(None, "tensor"),
            P("tensor", None),
            P(),
            P(None, "tensor"),
            P("tensor"),
            P("tensor", None),
            P(),
            P(),
            P(),
            P(),
            P(),
        ),
        check_vma=False,
    )
```

time: 673 us -> 462 us (0.69); the launches traced: 666 us -> 462 us
  Pallas kernels: 0 us -> 236 us
  matrix products: 156 us -> 0 us
  waiting for transfers between devices: 267 us -> 120 us
  blocking collectives: 81.1 us -> 0 us
  starting transfers between devices: 0.63 us -> 65.7 us
  other arithmetic: 71 us -> 15.9 us
  local copies, waits for them, and re-layouts: 74.2 us -> 21.4 us
  between operations: 15.3 us -> 2.3 us
    psum x4 -> x0, waiting for transfers between devices: 267 us -> none  [the longest x1 211 us: per_device(): lax.psum((grad_w_qkv, grad_b_qkv, grad_w_out, grad_b_out, grad_gain_one,...]
    pallas_call x0 -> x10, Pallas kernels: none -> 236 us  [the longest x3 155 us: assemble(): pl.pallas_call(functools.partial(assemble_kernel, kind, count), in_specs=...]
    dot_general x26 -> x0, matrix products: 156 us -> none  [the longest x2 27.2 us: one_block(): jnp.einsum('qhd,khd->hqk', grad_block, value_rows, preferred_element_type...]
    ppermute x0 -> x56, waiting for transfers between devices: none -> 120 us  [the longest x52 117 us: flip(): return lax.ppermute(values, 'dp', [(i, i ^ 1 << bit) for i in range(size)])]
    psum x1 -> x0, blocking collectives: 81.1 us -> none  [per_device(): lax.psum((grad_w_qkv, grad_b_qkv, grad_w_out, grad_b_out, grad_gain_one,...]
    ppermute x0 -> x56, starting transfers between devices: none -> 65.7 us  [the longest x52 65.1 us: flip(): return lax.ppermute(values, 'dp', [(i, i ^ 1 << bit) for i in range(size)])]
    convert_element_type x5 -> x1, other arithmetic: 35 us -> 4.14 us  [per_device(): outputs = (resid + (down + down_other + b_down)).astype(bf16)]
    dynamic_update_slice x4 -> x0, local copies, waits for them, and re-layouts: 30.7 us -> none  [attend_sequence(): attended, log_norm = lax.map(one_block, query_blocks)]
  transfers between devices with their start and end apart: 4 -> 56, of which waited for: 4 -> 23; matrix products, arithmetic and copies ran while one was open for 5% -> 4% of each run, Pallas kernels for 0% -> 28%
where the time goes in v1:
time: 462 us
  Pallas kernels  236 us (51%)
  waiting for transfers between devices  120 us (26%)
  starting transfers between devices  65.7 us (14%)
  local copies, waits for them, and re-layouts  21.4 us (5%)
  other arithmetic  15.9 us (3%)
    pallas_call x3, Pallas kernels, assemble(): pl.pallas_call(functools.partial(assemble_kernel, kind, count), in_specs=...  155 us
    ppermute x52, waiting for transfers between devices, flip(): return lax.ppermute(values, 'dp', [(i, i ^ 1 << bit) for i in range(size)])  117 us
    ppermute x52, starting transfers between devices, flip(): return lax.ppermute(values, 'dp', [(i, i ^ 1 << bit) for i in range(size)])  65.1 us
    pallas_call x2, Pallas kernels, attend_back(): pl.pallas_call(functools.partial(attend_back_kernel, first, count), grid=...  33.1 us
    pallas_call x2, Pallas kernels, mlp(): pl.pallas_call(functools.partial(mlp_kernel, first, count), grid=(rows //...  24.7 us
    unnamed x90, local copies, waits for them, and re-layouts  17.6 us
    pallas_call x1, Pallas kernels, front(): pl.pallas_call(functools.partial(front_kernel, block, steps), grid=(steps...  16 us
    concatenate x18, other arithmetic, gather(): own = jnp.concatenate([own, flip(own, bit, self.size)], axis=0)  10.5 us
  transfers between devices with their start and end apart: 56, of which 23 were waited for; matrix products, arithmetic and copies ran while one was open for 4% of the time, Pallas kernels for 28%

profile of v1, /device:TPU:0, one launch (start us, length us, event | category | flops | bytes accessed | tf_op | source)
XLA Modules:
  0.0 461.5 jit_solution(517924728747019845)
XLA Ops:
  9.3 16.0 %front.1 = (bf16[1024,640]{1,0:T(8,128)(2,1)S(1)}, bf16[320,1024]{1,0:T(8,128)(2,1)S(1)}, bf16[320,1024]{1,0:T(8,128)(2,1)S(1)}, bf16[320,1024]{1,0:T(8,128)(2,1...) custom-call(s32[1]{0:T(128)S(6)} %copy.34.length_ref, ...), custom_call_target="tpu_custom_call" | custom-call | flops 20000000000 | bytes 10485760 | tf_op jit(solution)/shard_map/front/pallas_call | solution.py:219
  31.4 3.6 collective-permute-done.refs_3_
  40.5 13.1 %mlp_a.1 = (f32[1024,640]{1,0:T(8,128)S(1)}, bf16[1024,640]{1,0:T(8,128)(2,1)S(1)}, f32[1024,640]{1,0:T(8,128)}, f32[1024,640]{1,0:T(8,128)}, f32[320,640]{1,0:T...) custom-call(s32[2]{0:T(128)S(1)} %pad_add_fusion.refs_0_.me_ref, ...), custom_call_target="tpu_custom_call" | custom-call | flops 5033164800 | bytes 20971520 | tf_op jit(solution)/shard_map/mlp_a/pallas_call | solution.py:339
  53.6 2.9 collective-permute-start.24
  58.0 11.6 %mlp_b.1 = (f32[1024,640]{1,0:T(8,128)}, f32[1024,640]{1,0:T(8,128)S(1)}, f32[320,640]{1,0:T(8,128)S(1)}, f32[320,640]{1,0:T(8,128)S(1)}, f32[320,640]{1,0:T(8,1...) custom-call(s32[2]{0:T(128)S(1)} %pad_add_fusion.1.refs_0_.me_ref, ...), custom_call_target="tpu_custom_call" | custom-call | flops 5033164800 | bytes 20971520 | tf_op jit(solution)/shard_map/mlp_b/pallas_call | solution.py:339
  70.3 5.5 %collective-permute-done.24 = f32[320,640]{1,0:T(8,128)S(1)} collective-permute-done((f32[320,640]{1,0:T(8,128)}, f32[320,640]{1,0:T(8,128)S(1)}, u32[]{:S(2)}, u32[]{:S(2)}) %collective-permute-start.24) | collective-permute-done | bytes 819232 | tf_op jit(solution)/shard_map/ppermute | solution.py:579
  75.9 2.1 collective-permute-start.25
  79.7 15.7 %collective-permute-done.32 = f32[320,640]{1,0:T(8,128)S(1)} collective-permute-done((f32[320,640]{1,0:T(8,128)S(1)}, f32[320,640]{1,0:T(8,128)S(1)}, u32[]{:S(2)}, u32[]{:S(2)}) %collective-permute-start.32) | collective-permute-done | bytes 819232 | tf_op jit(solution)/shard_map/ppermute | solution.py:579
  95.8 2.0 collective-permute-start.49
  97.8 6.4 %collective-permute-done.25 = f32[160,640]{1,0:T(8,128)S(1)} collective-permute-done((f32[160,640]{1,0:T(8,128)S(1)}, f32[160,640]{1,0:T(8,128)S(1)}, u32[]{:S(2)}, u32[]{:S(2)}) %collective-permute-start.25) | collective-permute-done | bytes 409632 | tf_op jit(solution)/shard_map/ppermute | solution.py:579
  106.5 3.9 collective-permute-done.33
  110.5 1.9 collective-permute-start.34
  113.6 2.7 collective-permute-start.27
  117.2 6.0 %collective-permute-done.34 = f32[80,640]{1,0:T(8,128)S(1)} collective-permute-done((f32[80,640]{1,0:T(8,128)S(1)}, f32[80,640]{1,0:T(8,128)S(1)}, u32[]{:S(2)}, u32[]{:S(2)}) %collective-permute-start.34) | collective-permute-done | bytes 204832 | tf_op jit(solution)/shard_map/ppermute | solution.py:579
  123.2 1.8 collective-permute-start.35
  125.0 2.3 collective-permute-done.50
  128.7 1.8 collective-permute-start.28
  131.8 3.6 middle.1
  135.6 16.4 %attend_back_a.1 = (f32[320,640]{1,0:T(8,128)S(1)}, f32[320,640]{1,0:T(8,128)S(1)}, f32[1024,640]{1,0:T(8,128)S(1)}, f32[8,480]{1,0:T(8,128)S(1)}) custom-call(s32[1]{0:T(128)} %bitcast.refs_0_, bf16[320,1024]{1,0:T(8,128)(2,1)S(1)} %copy-done.22, bf16[320,1024]{1,0:T(8,128)(2,1)S(1)} %copy-done.24, bf16[320,1024]{1,0:T(8,128)(2,1)S(1)} %copy-done.26, ...), custom_call_target="tpu_custom_call" | custom-call | flops 14000000000 | bytes 10485760 | tf_op jit(solution)/shard_map/attend_back_a/pallas_call | solution.py:525
  152.0 16.7 %attend_back_b.1 = (f32[320,640]{1,0:T(8,128)S(1)}, f32[320,640]{1,0:T(8,128)S(1)}, f32[1024,640]{1,0:T(8,128)S(1)}, f32[8,480]{1,0:T(8,128)S(1)}) custom-call(s32[1]{0:T(128)} %bitcast.1.refs_0_, bf16[320,1024]{1,0:T(8,128)(2,1)S(1)} %copy-done.22, bf16[320,1024]{1,0:T(8,128)(2,1)S(1)} %copy-done.24, bf16[320,1024]{1,0:T(8,128)(2,1)S(1)} %copy-done.26, ...), custom_call_target="tpu_custom_call" | custom-call | flops 14000000000 | bytes 10485760 | tf_op jit(solution)/shard_map/attend_back_b/pallas_call | solution.py:525
  173.2 1.8 collective-permute-start.52
  175.0 2.6 collective-permute-start.29
  178.3 2.7 collective-permute-done.52
  181.0 6.1 %collective-permute-done.12 = f32[320,640]{1,0:T(8,128)S(1)} collective-permute-done((f32[320,640]{1,0:T(8,128)S(1)}, f32[320,640]{1,0:T(8,128)S(1)}, u32[]{:S(2)}, u32[]{:S(2)}) %collective-permute-start.12) | collective-permute-done | bytes 819232 | tf_op jit(solution)/shard_map/ppermute | solution.py:579
  187.1 2.7 collective-permute-start.37
  191.9 3.6 collective-permute-done.37
  195.5 2.2 collective-permute-done.53
  199.3 2.6 collective-permute-start.46
  202.0 5.9 %collective-permute-done.5 = f32[160,640]{1,0:T(8,128)S(1)} collective-permute-done((f32[160,640]{1,0:T(8,128)S(1)}, f32[160,640]{1,0:T(8,128)S(1)}, u32[]{:S(2)}, u32[]{:S(2)}) %collective-permute-start.5) | collective-permute-done | bytes 409632 | tf_op jit(solution)/shard_map/ppermute | solution.py:579
  208.9 4.7 %collective-permute-done.14 = f32[80,640]{1,0:T(8,128)S(1)} collective-permute-done((f32[80,640]{1,0:T(8,128)S(1)}, f32[80,640]{1,0:T(8,128)S(1)}, u32[]{:S(2)}, u32[]{:S(2)}) %collective-permute-start.14) | collective-permute-done | bytes 204832 | tf_op jit(solution)/shard_map/ppermute | solution.py:579
  214.8 5.6 %collective-permute-done.6 = f32[80,640]{1,0:T(8,128)S(1)} collective-permute-done((f32[80,640]{1,0:T(8,128)S(1)}, f32[80,640]{1,0:T(8,128)S(1)}, u32[]{:S(2)}, u32[]{:S(2)}) %collective-permute-start.6) | collective-permute-done | bytes 204832 | tf_op jit(solution)/shard_map/ppermute | solution.py:579
  221.8 5.2 %collective-permute-done.15 = f32[40,640]{1,0:T(8,128)S(1)} collective-permute-done((f32[40,640]{1,0:T(8,128)S(1)}, f32[40,640]{1,0:T(8,128)S(1)}, u32[]{:S(2)}, u32[]{:S(2)}) %collective-permute-start.15) | collective-permute-done | bytes 102432 | tf_op jit(solution)/shard_map/ppermute | solution.py:579
  228.4 5.8 %collective-permute-done.7 = f32[40,640]{1,0:T(8,128)S(1)} collective-permute-done((f32[40,640]{1,0:T(8,128)S(1)}, f32[40,640]{1,0:T(8,128)S(1)}, u32[]{:S(2)}, u32[]{:S(2)}) %collective-permute-start.7) | collective-permute-done | bytes 102432 | tf_op jit(solution)/shard_map/ppermute | solution.py:579
  234.2 6.2 %collective-permute-done.16 = f32[40,640]{1,0:T(8,128)S(1)} collective-permute-done((f32[40,640]{1,0:T(8,128)S(1)}, f32[40,640]{1,0:T(8,128)S(1)}, u32[]{:S(2)}, u32[]{:S(2)}) %collective-permute-start.16) | collective-permute-done | bytes 102432 | tf_op jit(solution)/shard_map/ppermute | solution.py:579
  240.5 1.8 collective-permute-start.54
  242.3 3.8 collective-permute-done.8
  249.5 2.4 collective-permute-done.17
  255.5 3.3 last.1
  261.9 14.0 %collective-permute-done.20 = f32[10,640]{1,0:T(8,128)S(1)} collective-permute-done((f32[10,640]{1,0:T(8,128)S(1)}, f32[10,640]{1,0:T(8,128)S(1)}, u32[]{:S(2)}, u32[]{:S(2)}) %collective-permute-start.20) | collective-permute-done | bytes 25632 | tf_op jit(solution)/shard_map/ppermute | solution.py:579
  281.3 7.5 %collective-permute-done.21 = f32[10,640]{1,0:T(8,128)S(1)} collective-permute-done((f32[10,640]{1,0:T(8,128)S(1)}, f32[10,640]{1,0:T(8,128)S(1)}, u32[]{:S(2)}, u32[]{:S(2)}) %collective-permute-start.21) | collective-permute-done | bytes 25632 | tf_op jit(solution)/shard_map/ppermute | solution.py:579
  288.9 2.0 collective-permute-start.47
  291.4 2.3 collective-permute-start.22
  293.7 1.9 pad_maximum_fusion.refs_0_
  297.0 2.7 collective-permute-start.23
  299.8 4.1 add_convert_fusion
  303.9 76.4 %assemble_up.1 = f32[640,1280]{1,0:T(8,128)} custom-call(s32[2]{0:T(128)S(1)} %pad_add_fusion.1.refs_0_.me_ref, f32[320,640]{1,0:T(8,128)} %pad_maximum_fusion.2.refs_0_, f32[320,640]{1,0:T(8,128)} %collective-permute-done.31.refs_1_, f32[320,640]{1,0:T(8,128)} %pad_maximum_fusion.3.refs_2_, f32[320,640]{1,0:T(8,128)S(1)} %collective-permute-done.39.refs_3_), custom_call_target="tpu_custom_call" | custom-call | bytes 7340032 | tf_op jit(solution)/shard_map/assemble_up/pallas_call | solution.py:657
  380.3 2.5 assemble_down.1
  384.9 76.4 %assemble_attention.1 = (f32[960,640]{1,0:T(8,128)}, f32[320,640]{1,0:T(8,128)}) custom-call(s32[2]{0:T(128)S(1)} %pad_add_fusion.refs_0_.me_ref, f32[320,640]{1,0:T(8,128)} %pad_maximum_fusion.refs_0_, f32[320,640]{1,0:T(8,128)} %collective-permute-done.11.refs_1_, f32[320,640]{1,0:T(8,128)S(1)} %pad_maximum_fusion.1.refs_2_, ...), custom_call_target="tpu_custom_call" | custom-call | bytes 7340032 | tf_op jit(solution)/shard_map/assemble_attention/pallas_call | solution.py:657
  (251 shorter events, 64.1 us)
Async XLA Ops:
  53.6 22.2 %collective-permute-start.24 = (f32[320,640]{1,0:T(8,128)}, f32[320,640]{1,0:T(8,128)S(1)}, u32[]{:S(2)}, u32[]{:S(2)}) collective-permute-start(f32[320,640]{1,0:T(8,128)} %get-tuple-element.87), channel_id=1, source_target_pairs={{0,4},{2,6},{4,0},{6,2},{8,12},{10,14},{12,8},{14,10},{16,20},{18,... | collective-permute-start | bytes 2457608 | tf_op jit(solution)/shard_map/ppermute | solution.py:579
  56.5 21.5 %collective-permute-start.40 = (f32[320,640]{1,0:T(8,128)}, f32[320,640]{1,0:T(8,128)S(1)}, u32[]{:S(2)}, u32[]{:S(2)}) collective-permute-start(f32[320,640]{1,0:T(8,128)} %get-tuple-element.91), channel_id=1, source_target_pairs={{0,2},{2,0},{4,6},{6,4},{8,10},{10,8},{12,14},{14,12},{16,18},{18,... | collective-permute-start | bytes 2457608 | tf_op jit(solution)/shard_map/ppermute | solution.py:579
  69.6 25.8 %collective-permute-start.32 = (f32[320,640]{1,0:T(8,128)S(1)}, f32[320,640]{1,0:T(8,128)S(1)}, u32[]{:S(2)}, u32[]{:S(2)}) collective-permute-start(f32[320,640]{1,0:T(8,128)S(1)} %get-tuple-element.89), channel_id=1, source_target_pairs={{0,2},{2,0},{4,6},{6,4},{8,10},{10,8},{12,14},{14,12},{16,18},{18,... | collective-permute-start | bytes 2457608 | tf_op jit(solution)/shard_map/ppermute | solution.py:579
  70.2 25.5 %collective-permute-start.48 = (f32[320,640]{1,0:T(8,128)S(1)}, f32[320,640]{1,0:T(8,128)S(1)}, u32[]{:S(2)}, u32[]{:S(2)}) collective-permute-start(f32[320,640]{1,0:T(8,128)S(1)} %get-tuple-element.93), channel_id=1, source_target_pairs={{0,4},{2,6},{4,0},{6,2},{8,12},{10,14},{12,8},{14,10},{16,20},{18,... | collective-permute-start | bytes 2457608 | tf_op jit(solution)/shard_map/ppermute | solution.py:579
  75.9 28.3 %collective-permute-start.25 = (f32[160,640]{1,0:T(8,128)S(1)}, f32[160,640]{1,0:T(8,128)S(1)}, u32[]{:S(2)}, u32[]{:S(2)}) collective-permute-start(f32[160,640]{1,0:T(8,128)S(1)} %slice.207), channel_id=1, source_target_pairs={{0,2},{2,0},{4,6},{6,4},{8,10},{10,8},{12,14},{14,12},{16,18},{18,... | collective-permute-start | bytes 1228808 | tf_op jit(solution)/shard_map/ppermute | solution.py:579
  78.0 53.8 %collective-permute-start.2 = (f32[1024,640]{1,0:T(8,128)S(1)}, f32[1024,640]{1,0:T(8,128)S(1)}, u32[]{:S(2)}, u32[]{:S(2)}) collective-permute-start(f32[1024,640]{1,0:T(8,128)S(1)} %get-tuple-element.64.own_ref), channel_id=1, source_target_pairs={{0,1},{1,0},{2,3},{3,2},{4,5},{5,4},{6,7},{7,6},{8,9},{9,8},{10,11... | collective-permute-start | bytes 7864328 | tf_op jit(solution)/shard_map/ppermute | solution.py:706
  78.1 27.8 %collective-permute-start.41 = (f32[160,640]{1,0:T(8,128)S(1)}, f32[160,640]{1,0:T(8,128)S(1)}, u32[]{:S(2)}, u32[]{:S(2)}) collective-permute-start(f32[160,640]{1,0:T(8,128)S(1)} %slice.220), channel_id=1, source_target_pairs={{0,4},{2,6},{4,0},{6,2},{8,12},{10,14},{12,8},{14,10},{16,20},{18,... | collective-permute-start | bytes 1228808 | tf_op jit(solution)/shard_map/ppermute | solution.py:579
  95.6 14.9 %collective-permute-start.33 = (f32[160,640]{1,0:T(8,128)S(1)}, f32[160,640]{1,0:T(8,128)S(1)}, u32[]{:S(2)}, u32[]{:S(2)}) collective-permute-start(f32[160,640]{1,0:T(8,128)S(1)} %slice.213), channel_id=1, source_target_pairs={{0,4},{2,6},{4,0},{6,2},{8,12},{10,14},{12,8},{14,10},{16,20},{18,... | collective-permute-start | bytes 1228808 | tf_op jit(solution)/shard_map/ppermute | solution.py:579
  95.8 16.5 %collective-permute-start.49 = (f32[160,640]{1,0:T(8,128)S(1)}, f32[160,640]{1,0:T(8,128)S(1)}, u32[]{:S(2)}, u32[]{:S(2)}) collective-permute-start(f32[160,640]{1,0:T(8,128)S(1)} %slice.226), channel_id=1, source_target_pairs={{0,2},{2,0},{4,6},{6,4},{8,10},{10,8},{12,14},{14,12},{16,18},{18,... | collective-permute-start | bytes 1228808 | tf_op jit(solution)/shard_map/ppermute | solution.py:579
  104.3 9.3 %collective-permute-start.26 = (f32[80,640]{1,0:T(8,128)S(1)}, f32[80,640]{1,0:T(8,128)S(1)}, u32[]{:S(2)}, u32[]{:S(2)}) collective-permute-start(f32[80,640]{1,0:T(8,128)S(1)} %slice.209), channel_id=1, source_target_pairs={{0,8},{2,10},{4,12},{6,14},{8,0},{10,2},{12,4},{14,6},{16,24},{18,... | collective-permute-start | bytes 614408 | tf_op jit(solution)/shard_map/ppermute | solution.py:579
  106.0 10.3 %collective-permute-start.42 = (f32[80,640]{1,0:T(8,128)S(1)}, f32[80,640]{1,0:T(8,128)S(1)}, u32[]{:S(2)}, u32[]{:S(2)}) collective-permute-start(f32[80,640]{1,0:T(8,128)S(1)} %slice.222), channel_id=1, source_target_pairs={{0,8},{2,10},{4,12},{6,14},{8,0},{10,2},{12,4},{14,6},{16,24},{18,... | collective-permute-start | bytes 614408 | tf_op jit(solution)/shard_map/ppermute | solution.py:579
  110.5 12.6 %collective-permute-start.34 = (f32[80,640]{1,0:T(8,128)S(1)}, f32[80,640]{1,0:T(8,128)S(1)}, u32[]{:S(2)}, u32[]{:S(2)}) collective-permute-start(f32[80,640]{1,0:T(8,128)S(1)} %slice.215), channel_id=1, source_target_pairs={{0,8},{2,10},{4,12},{6,14},{8,0},{10,2},{12,4},{14,6},{16,24},{18,... | collective-permute-start | bytes 614408 | tf_op jit(solution)/shard_map/ppermute | solution.py:579
  112.4 14.9 %collective-permute-start.50 = (f32[80,640]{1,0:T(8,128)S(1)}, f32[80,640]{1,0:T(8,128)S(1)}, u32[]{:S(2)}, u32[]{:S(2)}) collective-permute-start(f32[80,640]{1,0:T(8,128)S(1)} %slice.228), channel_id=1, source_target_pairs={{0,8},{2,10},{4,12},{6,14},{8,0},{10,2},{12,4},{14,6},{16,24},{18,... | collective-permute-start | bytes 614408 | tf_op jit(solution)/shard_map/ppermute | solution.py:579
  113.6 15.0 %collective-permute-start.27 = (f32[40,640]{1,0:T(8,128)S(1)}, f32[40,640]{1,0:T(8,128)S(1)}, u32[]{:S(2)}, u32[]{:S(2)}) collective-permute-start(f32[40,640]{1,0:T(8,128)S(1)} %slice.211), channel_id=1, source_target_pairs={{0,16},{2,18},{4,20},{6,22},{8,24},{10,26},{12,28},{14,30},{16,0},... | collective-permute-start | bytes 307208 | tf_op jit(solution)/shard_map/ppermute | solution.py:579
  116.3 14.1 %collective-permute-start.43 = (f32[40,640]{1,0:T(8,128)S(1)}, f32[40,640]{1,0:T(8,128)S(1)}, u32[]{:S(2)}, u32[]{:S(2)}) collective-permute-start(f32[40,640]{1,0:T(8,128)S(1)} %slice.224), channel_id=1, source_target_pairs={{0,16},{2,18},{4,20},{6,22},{8,24},{10,26},{12,28},{14,30},{16,0},... | collective-permute-start | bytes 307208 | tf_op jit(solution)/shard_map/ppermute | solution.py:579
  123.2 47.2 %collective-permute-start.35 = (f32[40,640]{1,0:T(8,128)S(1)}, f32[40,640]{1,0:T(8,128)S(1)}, u32[]{:S(2)}, u32[]{:S(2)}) collective-permute-start(f32[40,640]{1,0:T(8,128)S(1)} %slice.217), channel_id=1, source_target_pairs={{0,16},{2,18},{4,20},{6,22},{8,24},{10,26},{12,28},{14,30},{16,0},... | collective-permute-start | bytes 307208 | tf_op jit(solution)/shard_map/ppermute | solution.py:579
  127.4 44.4 %collective-permute-start.51 = (f32[40,640]{1,0:T(8,128)S(1)}, f32[40,640]{1,0:T(8,128)S(1)}, u32[]{:S(2)}, u32[]{:S(2)}) collective-permute-start(f32[40,640]{1,0:T(8,128)S(1)} %slice.230), channel_id=1, source_target_pairs={{0,16},{2,18},{4,20},{6,22},{8,24},{10,26},{12,28},{14,30},{16,0},... | collective-permute-start | bytes 307208 | tf_op jit(solution)/shard_map/ppermute | solution.py:579
  128.7 44.5 %collective-permute-start.28 = (f32[40,640]{1,0:T(8,128)S(1)}, f32[40,640]{1,0:T(8,128)S(1)}, u32[]{:S(2)}, u32[]{:S(2)}) collective-permute-start(f32[40,640]{1,0:T(8,128)S(1)} %slice_add_fusion.15), channel_id=1, source_target_pairs={{0,16},{2,18},{4,20},{6,22},{8,24},{10,26},{12,28},{14,30},{16,0},... | collective-permute-start | bytes 307208 | tf_op jit(solution)/shard_map/ppermute | solution.py:579
  130.5 44.5 %collective-permute-start.44 = (f32[40,640]{1,0:T(8,128)S(1)}, f32[40,640]{1,0:T(8,128)S(1)}, u32[]{:S(2)}, u32[]{:S(2)}) collective-permute-start(f32[40,640]{1,0:T(8,128)S(1)} %slice_add_fusion.13), channel_id=1, source_target_pairs={{0,16},{2,18},{4,20},{6,22},{8,24},{10,26},{12,28},{14,30},{16,0},... | collective-permute-start | bytes 307208 | tf_op jit(solution)/shard_map/ppermute | solution.py:579
  168.7 18.4 %collective-permute-start.12 = (f32[320,640]{1,0:T(8,128)S(1)}, f32[320,640]{1,0:T(8,128)S(1)}, u32[]{:S(2)}, u32[]{:S(2)}) collective-permute-start(f32[320,640]{1,0:T(8,128)S(1)} %get-tuple-element.77), channel_id=1, source_target_pairs={{0,4},{2,6},{4,0},{6,2},{8,12},{10,14},{12,8},{14,10},{16,20},{18,... | collective-permute-start | bytes 2457608 | tf_op jit(solution)/shard_map/ppermute | solution.py:579
  170.4 7.8 %collective-permute-start.36 = (f32[40,640]{1,0:T(8,128)S(1)}, f32[40,640]{1,0:T(8,128)S(1)}, u32[]{:S(2)}, u32[]{:S(2)}) collective-permute-start(f32[40,640]{1,0:T(8,128)S(1)} %slice_add_fusion.14), channel_id=1, source_target_pairs={{0,16},{2,18},{4,20},{6,22},{8,24},{10,26},{12,28},{14,30},{16,0},... | collective-permute-start | bytes 307208 | tf_op jit(solution)/shard_map/ppermute | solution.py:579
  171.8 19.9 %collective-permute-start.4 = (f32[320,640]{1,0:T(8,128)S(1)}, f32[320,640]{1,0:T(8,128)S(1)}, u32[]{:S(2)}, u32[]{:S(2)}) collective-permute-start(f32[320,640]{1,0:T(8,128)S(1)} %get-tuple-element.75), channel_id=1, source_target_pairs={{0,2},{2,0},{4,6},{6,4},{8,10},{10,8},{12,14},{14,12},{16,18},{18,... | collective-permute-start | bytes 2457608 | tf_op jit(solution)/shard_map/ppermute | solution.py:579
  173.2 7.8 %collective-permute-start.52 = (f32[40,640]{1,0:T(8,128)S(1)}, f32[40,640]{1,0:T(8,128)S(1)}, u32[]{:S(2)}, u32[]{:S(2)}) collective-permute-start(f32[40,640]{1,0:T(8,128)S(1)} %slice_add_fusion.12), channel_id=1, source_target_pairs={{0,16},{2,18},{4,20},{6,22},{8,24},{10,26},{12,28},{14,30},{16,0},... | collective-permute-start | bytes 307208 | tf_op jit(solution)/shard_map/ppermute | solution.py:579
  175.0 14.9 %collective-permute-start.29 = (f32[80,640]{1,0:T(8,128)S(1)}, f32[80,640]{1,0:T(8,128)S(1)}, u32[]{:S(2)}, u32[]{:S(2)}) collective-permute-start(f32[80,640]{1,0:T(8,128)S(1)} %pad_maximum_fusion.14), channel_id=1, source_target_pairs={{0,8},{2,10},{4,12},{6,14},{8,0},{10,2},{12,4},{14,6},{16,24},{18,... | collective-permute-start | bytes 614408 | tf_op jit(solution)/shard_map/ppermute | solution.py:579
  178.2 74.5 %collective-permute-start.3 = (f32[1024,640]{1,0:T(8,128)S(1)}, f32[1024,640]{1,0:T(8,128)S(1)}, u32[]{:S(2)}, u32[]{:S(2)}) collective-permute-start(f32[1024,640]{1,0:T(8,128)S(1)} %get-tuple-element.71.own_ref), channel_id=1, source_target_pairs={{0,1},{1,0},{2,3},{3,2},{4,5},{5,4},{6,7},{7,6},{8,9},{9,8},{10,11... | collective-permute-start | bytes 7864328 | tf_op jit(solution)/shard_map/ppermute | solution.py:706
  181.0 10.6 %collective-permute-start.45 = (f32[80,640]{1,0:T(8,128)S(1)}, f32[80,640]{1,0:T(8,128)S(1)}, u32[]{:S(2)}, u32[]{:S(2)}) collective-permute-start(f32[80,640]{1,0:T(8,128)S(1)} %pad_maximum_fusion.16), channel_id=1, source_target_pairs={{0,8},{2,10},{4,12},{6,14},{8,0},{10,2},{12,4},{14,6},{16,24},{18,... | collective-permute-start | bytes 614408 | tf_op jit(solution)/shard_map/ppermute | solution.py:579
  187.1 8.4 %collective-permute-start.37 = (f32[80,640]{1,0:T(8,128)S(1)}, f32[80,640]{1,0:T(8,128)S(1)}, u32[]{:S(2)}, u32[]{:S(2)}) collective-permute-start(f32[80,640]{1,0:T(8,128)S(1)} %pad_maximum_fusion.15), channel_id=1, source_target_pairs={{0,8},{2,10},{4,12},{6,14},{8,0},{10,2},{12,4},{14,6},{16,24},{18,... | collective-permute-start | bytes 614408 | tf_op jit(solution)/shard_map/ppermute | solution.py:579
  189.9 9.4 %collective-permute-start.13 = (f32[160,640]{1,0:T(8,128)S(1)}, f32[160,640]{1,0:T(8,128)S(1)}, u32[]{:S(2)}, u32[]{:S(2)}) collective-permute-start(f32[160,640]{1,0:T(8,128)S(1)} %slice.199), channel_id=1, source_target_pairs={{0,2},{2,0},{4,6},{6,4},{8,10},{10,8},{12,14},{14,12},{16,18},{18,... | collective-permute-start | bytes 1228808 | tf_op jit(solution)/shard_map/ppermute | solution.py:579
  191.7 99.3 %collective-permute-start.1 = (f32[1024,640]{1,0:T(8,128)}, f32[1024,640]{1,0:T(8,128)}, u32[]{:S(2)}, u32[]{:S(2)}) collective-permute-start(f32[1024,640]{1,0:T(8,128)} %get-tuple-element.59), channel_id=1, source_target_pairs={{0,1},{1,0},{2,3},{3,2},{4,5},{5,4},{6,7},{7,6},{8,9},{9,8},{10,11... | collective-permute-start | bytes 7864328 | tf_op jit(solution)/shard_map/ppermute | solution.py:706
  195.5 12.4 %collective-permute-start.5 = (f32[160,640]{1,0:T(8,128)S(1)}, f32[160,640]{1,0:T(8,128)S(1)}, u32[]{:S(2)}, u32[]{:S(2)}) collective-permute-start(f32[160,640]{1,0:T(8,128)S(1)} %slice.193), channel_id=1, source_target_pairs={{0,4},{2,6},{4,0},{6,2},{8,12},{10,14},{12,8},{14,10},{16,20},{18,... | collective-permute-start | bytes 1228808 | tf_op jit(solution)/shard_map/ppermute | solution.py:579
  197.7 29.8 %collective-permute-start.30 = (f32[160,640]{1,0:T(8,128)S(1)}, f32[160,640]{1,0:T(8,128)S(1)}, u32[]{:S(2)}, u32[]{:S(2)}) collective-permute-start(f32[160,640]{1,0:T(8,128)S(1)} %pad_maximum_fusion.8), channel_id=1, source_target_pairs={{0,2},{2,0},{4,6},{6,4},{8,10},{10,8},{12,14},{14,12},{16,18},{18,... | collective-permute-start | bytes 1228808 | tf_op jit(solution)/shard_map/ppermute | solution.py:579
  199.3 41.2 %collective-permute-start.46 = (f32[160,640]{1,0:T(8,128)S(1)}, f32[160,640]{1,0:T(8,128)S(1)}, u32[]{:S(2)}, u32[]{:S(2)}) collective-permute-start(f32[160,640]{1,0:T(8,128)S(1)} %pad_maximum_fusion.10), channel_id=1, source_target_pairs={{0,4},{2,6},{4,0},{6,2},{8,12},{10,14},{12,8},{14,10},{16,20},{18,... | collective-permute-start | bytes 1228808 | tf_op jit(solution)/shard_map/ppermute | solution.py:579
  213.7 6.7 %collective-permute-start.6 = (f32[80,640]{1,0:T(8,128)S(1)}, f32[80,640]{1,0:T(8,128)S(1)}, u32[]{:S(2)}, u32[]{:S(2)}) collective-permute-start(f32[80,640]{1,0:T(8,128)S(1)} %slice.195), channel_id=1, source_target_pairs={{0,8},{2,10},{4,12},{6,14},{8,0},{10,2},{12,4},{14,6},{16,24},{18,... | collective-permute-start | bytes 614408 | tf_op jit(solution)/shard_map/ppermute | solution.py:579
  227.0 7.2 %collective-permute-start.7 = (f32[40,640]{1,0:T(8,128)S(1)}, f32[40,640]{1,0:T(8,128)S(1)}, u32[]{:S(2)}, u32[]{:S(2)}) collective-permute-start(f32[40,640]{1,0:T(8,128)S(1)} %slice.197), channel_id=1, source_target_pairs={{0,16},{2,18},{4,20},{6,22},{8,24},{10,26},{12,28},{14,30},{16,0},... | collective-permute-start | bytes 307208 | tf_op jit(solution)/shard_map/ppermute | solution.py:579
  227.5 20.3 %collective-permute-start.38 = (f32[160,640]{1,0:T(8,128)S(1)}, f32[160,640]{1,0:T(8,128)S(1)}, u32[]{:S(2)}, u32[]{:S(2)}) collective-permute-start(f32[160,640]{1,0:T(8,128)S(1)} %pad_maximum_fusion.9), channel_id=1, source_target_pairs={{0,4},{2,6},{4,0},{6,2},{8,12},{10,14},{12,8},{14,10},{16,20},{18,... | collective-permute-start | bytes 1228808 | tf_op jit(solution)/shard_map/ppermute | solution.py:579
  240.5 18.3 %collective-permute-start.54 = (f32[160,640]{1,0:T(8,128)}, f32[160,640]{1,0:T(8,128)}, u32[]{:S(2)}, u32[]{:S(2)}) collective-permute-start(f32[160,640]{1,0:T(8,128)} %pad_maximum_fusion.11), channel_id=1, source_target_pairs={{0,2},{2,0},{4,6},{6,4},{8,10},{10,8},{12,14},{14,12},{16,18},{18,... | collective-permute-start | bytes 1228808 | tf_op jit(solution)/shard_map/ppermute | solution.py:579
  247.8 47.8 %collective-permute-start.31 = (f32[320,640]{1,0:T(8,128)}, f32[320,640]{1,0:T(8,128)}, u32[]{:S(2)}, u32[]{:S(2)}) collective-permute-start(f32[320,640]{1,0:T(8,128)} %pad_maximum_fusion.2.refs_0_), channel_id=1, source_target_pairs={{0,4},{2,6},{4,0},{6,2},{8,12},{10,14},{12,8},{14,10},{16,20},{18,... | collective-permute-start | bytes 2457608 | tf_op jit(solution)/shard_map/ppermute | solution.py:579
  251.9 7.3 %collective-permute-start.9 = (f32[80,640]{1,0:T(8,128)}, f32[80,640]{1,0:T(8,128)}, u32[]{:S(2)}, u32[]{:S(2)}) collective-permute-start(f32[80,640]{1,0:T(8,128)} %pad_maximum_fusion.12), channel_id=1, source_target_pairs={{0,8},{2,10},{4,12},{6,14},{8,0},{10,2},{12,4},{14,6},{16,24},{18,... | collective-permute-start | bytes 614408 | tf_op jit(solution)/shard_map/ppermute | solution.py:579
  252.7 27.0 %collective-permute-start.18 = (f32[160,640]{1,0:T(8,128)}, f32[160,640]{1,0:T(8,128)}, u32[]{:S(2)}, u32[]{:S(2)}) collective-permute-start(f32[160,640]{1,0:T(8,128)} %pad_maximum_fusion.7), channel_id=1, source_target_pairs={{0,2},{2,0},{4,6},{6,4},{8,10},{10,8},{12,14},{14,12},{16,18},{18,... | collective-permute-start | bytes 1228808 | tf_op jit(solution)/shard_map/ppermute | solution.py:579
  258.9 38.2 %collective-permute-start.39 = (f32[320,640]{1,0:T(8,128)}, f32[320,640]{1,0:T(8,128)S(1)}, u32[]{:S(2)}, u32[]{:S(2)}) collective-permute-start(f32[320,640]{1,0:T(8,128)} %pad_maximum_fusion.3.refs_2_), channel_id=1, source_target_pairs={{0,2},{2,0},{4,6},{6,4},{8,10},{10,8},{12,14},{14,12},{16,18},{18,... | collective-permute-start | bytes 2457608 | tf_op jit(solution)/shard_map/ppermute | solution.py:579
  259.2 16.7 %collective-permute-start.20 = (f32[10,640]{1,0:T(8,128)S(1)}, f32[10,640]{1,0:T(8,128)S(1)}, u32[]{:S(2)}, u32[]{:S(2)}) collective-permute-start(f32[10,640]{1,0:T(8,128)S(1)} %concatenate.75), channel_id=1, source_target_pairs={{0,2},{2,0},{4,6},{6,4},{8,10},{10,8},{12,14},{14,12},{16,18},{18,... | collective-permute-start | bytes 76808 | tf_op jit(solution)/shard_map/ppermute | solution.py:579
  276.0 15.4 %collective-permute-start.10 = (f32[160,640]{1,0:T(8,128)S(1)}, f32[160,640]{1,0:T(8,128)S(1)}, u32[]{:S(2)}, u32[]{:S(2)}) collective-permute-start(f32[160,640]{1,0:T(8,128)S(1)} %pad_maximum_fusion.6), channel_id=1, source_target_pairs={{0,4},{2,6},{4,0},{6,2},{8,12},{10,14},{12,8},{14,10},{16,20},{18,... | collective-permute-start | bytes 1228808 | tf_op jit(solution)/shard_map/ppermute | solution.py:579
  279.7 9.1 %collective-permute-start.21 = (f32[10,640]{1,0:T(8,128)S(1)}, f32[10,640]{1,0:T(8,128)S(1)}, u32[]{:S(2)}, u32[]{:S(2)}) collective-permute-start(f32[10,640]{1,0:T(8,128)S(1)} %add.138), channel_id=1, source_target_pairs={{0,4},{2,6},{4,0},{6,2},{8,12},{10,14},{12,8},{14,10},{16,20},{18,... | collective-permute-start | bytes 76808 | tf_op jit(solution)/shard_map/ppermute | solution.py:579
  288.9 91.5 %collective-permute-start.47 = (f32[320,640]{1,0:T(8,128)S(1)}, f32[320,640]{1,0:T(8,128)S(1)}, u32[]{:S(2)}, u32[]{:S(2)}) collective-permute-start(f32[320,640]{1,0:T(8,128)S(1)} %pad_maximum_fusion.4.refs_0_), channel_id=1, source_target_pairs={{0,2},{2,0},{4,6},{6,4},{8,10},{10,8},{12,14},{14,12},{16,18},{18,... | collective-permute-start | bytes 2457608 | tf_op jit(solution)/shard_map/ppermute | solution.py:579
  290.9 89.4 %collective-permute-start.55 = (f32[320,640]{1,0:T(8,128)S(1)}, f32[320,640]{1,0:T(8,128)S(1)}, u32[]{:S(2)}, u32[]{:S(2)}) collective-permute-start(f32[320,640]{1,0:T(8,128)S(1)} %pad_maximum_fusion.5.refs_2_), channel_id=1, source_target_pairs={{0,4},{2,6},{4,0},{6,2},{8,12},{10,14},{12,8},{14,10},{16,20},{18,... | collective-permute-start | bytes 2457608 | tf_op jit(solution)/shard_map/ppermute | solution.py:579
  295.6 89.3 %collective-permute-start.19 = (f32[320,640]{1,0:T(8,128)S(1)}, f32[320,640]{1,0:T(8,128)}, u32[]{:S(2)}, u32[]{:S(2)}) collective-permute-start(f32[320,640]{1,0:T(8,128)S(1)} %pad_maximum_fusion.1.refs_2_), channel_id=1, source_target_pairs={{0,4},{2,6},{4,0},{6,2},{8,12},{10,14},{12,8},{14,10},{16,20},{18,... | collective-permute-start | bytes 2457608 | tf_op jit(solution)/shard_map/ppermute | solution.py:579
  297.0 87.9 %collective-permute-start.11 = (f32[320,640]{1,0:T(8,128)}, f32[320,640]{1,0:T(8,128)}, u32[]{:S(2)}, u32[]{:S(2)}) collective-permute-start(f32[320,640]{1,0:T(8,128)} %pad_maximum_fusion.refs_0_), channel_id=1, source_target_pairs={{0,2},{2,0},{4,6},{6,4},{8,10},{10,8},{12,14},{14,12},{16,18},{18,... | collective-permute-start | bytes 2457608 | tf_op jit(solution)/shard_map/ppermute | solution.py:579
  297.0 85.8 %collective-permute-start.23 = (f32[10,640]{1,0:T(8,128)S(1)}, f32[10,640]{1,0:T(8,128)S(1)}, u32[]{:S(2)}, u32[]{:S(2)}) collective-permute-start(f32[10,640]{1,0:T(8,128)S(1)} %add.140), channel_id=1, source_target_pairs={{0,16},{2,18},{4,20},{6,22},{8,24},{10,26},{12,28},{14,30},{16,0},... | collective-permute-start | bytes 76808 | tf_op jit(solution)/shard_map/ppermute | solution.py:579
  (53 other events, 528.0 us)
